TPU v7x, 1024 devices: a whole 4x4x32 slice. The times are simulated.
1024 devices in a mesh: seq: 32 (over z), uly: 8 (over y_lo, x), rep: 4 (over y_hi, core).
Axes of the slice: x: 4, y: 4 (y_hi: 2, y_lo: 2; y = y_hi * 2 + y_lo), z: 32, core: 2. Of those that a mesh axis runs over, the one named last changes fastest.
Arguments:
- queries: bfloat16 [131072, 2048], P(('rep', 'seq', 'uly')), parts along dimension 0, may hold values from -6 to 6
- keys: bfloat16 [131072, 2048], P(('rep', 'seq', 'uly')), parts along dimension 0, may hold values from -6 to 6
- values: bfloat16 [131072, 2048], P(('rep', 'seq', 'uly')), parts along dimension 0, may hold values from -6 to 6
- past_outputs: bfloat16 [2, 131072, 2048], P(None, ('rep', 'seq', 'uly')), parts along dimension 1, may hold values from -6 to 6
- dwa_slot: int32 [2], replicated, may hold values from 0 to 63
- dwa_table: float32 [2, 64], replicated, may hold values from 0.1 to 0.6
Outputs:
- mixed: bfloat16 [131072, 2048], P(('rep', 'seq', 'uly')), parts along dimension 0
There are 4 independent parts, one for each index of `rep`. A program takes and returns all parts, laid end to end along the dimension named above; an argument that names none is the same for every part. Nothing has to cross between parts.
All inputs are finite; a program needn't handle non-finite values.
Results may differ from a plain program's by a relative error of at most 0.0034.
Values may be sent and summed in bfloat16 or wider, within the bound.
A program may use at most 64 MiB of HBM per device.

v0:
```python
import jax
import jax.numpy as jnp
from jax import lax
from jax.sharding import PartitionSpec as P

HEAD_DIM = 128


def from_behind(block, axis, distance):
    devices = range(lax.axis_size(axis))
    route = [(i - distance, i) for i in devices if i - distance in devices]
    return lax.ppermute(block, axis, route)


def block_update(state, query_heads, key_heads, value_heads, allowed):
    running, total, accumulated = state
    scores = jnp.einsum("qhd,khd->hqk", query_heads, key_heads, preferred_element_type=jnp.float32)
    scores = scores * (1.0 / HEAD_DIM**0.5)
    scores = jnp.where(allowed, scores, -jnp.inf)
    new_max = jnp.maximum(running, jnp.max(scores, axis=2))
    factor = jnp.exp(running - new_max)
    prob = jnp.exp(scores - new_max[:, :, None])
    total = total * factor + jnp.sum(prob, axis=2)
    weights = prob.astype(jnp.bfloat16)
    update = jnp.einsum("hqk,khd->qhd", weights, value_heads, preferred_element_type=jnp.float32)
    accumulated = accumulated * jnp.transpose(factor)[:, :, None] + update
    return (new_max, total, accumulated)


def shards(queries, keys, values, past_outputs, dwa_slot, dwa_table):
    n_uly = lax.axis_size("uly")
    n_seq = lax.axis_size("seq")
    span_size = min(4, n_seq)
    features = queries.shape[1]
    local_heads = features // n_uly // HEAD_DIM
    query_rows, key_rows, value_rows = (
        lax.all_to_all(queries, "uly", split_axis=1, concat_axis=0, tiled=True),
        lax.all_to_all(keys, "uly", split_axis=1, concat_axis=0, tiled=True),
        lax.all_to_all(values, "uly", split_axis=1, concat_axis=0, tiled=True),
    )
    row_count = query_rows.shape[0]
    split_shape = (row_count, local_heads, HEAD_DIM)
    query_heads = query_rows.reshape(split_shape)
    table_index = jnp.arange(dwa_table.shape[1])
    onehot = (dwa_slot[:, None] == table_index[None, :]).astype(jnp.float32)
    coefs = jnp.dot(onehot, jnp.transpose(dwa_table), precision=lax.Precision.HIGHEST)
    layer_in = jnp.zeros(queries.shape, jnp.float32)
    extra = jnp.zeros(queries.shape, jnp.float32)
    for index in range(past_outputs.shape[0]):
        stored = past_outputs[index].astype(jnp.float32)
        layer_in = layer_in + coefs[index, 0] * stored
        extra = extra + coefs[index, 1] * stored
    running = jnp.full((local_heads, row_count), -jnp.inf, jnp.float32)
    total = jnp.zeros((local_heads, row_count), jnp.float32)
    accumulated = jnp.zeros(split_shape, jnp.float32)
    state = (running, total, accumulated)
    causal = (jnp.arange(row_count)[:, None] >= jnp.arange(row_count)[None, :])[None, :, :]
    state = block_update(
        state, query_heads, key_rows.reshape(split_shape), value_rows.reshape(split_shape), causal
    )
    position = lax.axis_index("seq")
    current = (key_rows, value_rows)
    for offset in range(1, span_size):
        current = from_behind((current[0], current[1]), "seq", 1)
        far_keys = current[0].reshape(split_shape)
        far_values = current[1].reshape(split_shape)

        def take_block(carry, far_keys=far_keys, far_values=far_values):
            return block_update(carry, query_heads, far_keys, far_values, True)

        def keep_block(carry):
            return carry

        state = lax.cond(position >= offset, take_block, keep_block, state)
    running, total, accumulated = state
    attended = accumulated / jnp.transpose(total)[:, :, None]
    attended = attended.astype(jnp.bfloat16).reshape(row_count, local_heads * HEAD_DIM)
    returned = lax.all_to_all(attended, "uly", split_axis=0, concat_axis=1, tiled=True)
    hidden = layer_in + returned.astype(jnp.float32)
    return (hidden + extra).astype(jnp.bfloat16)


def solution(mesh):
    return jax.shard_map(
        shards,
        mesh=mesh,
        in_specs=(
            P(("rep", "seq", "uly"), None),
            P(("rep", "seq", "uly"), None),
            P(("rep", "seq", "uly"), None),
            P(None, ("rep", "seq", "uly"), None),
            P(),
            P(),
        ),
        out_specs=P(("rep", "seq", "uly"), None),
        check_vma=False,
    )
```

profile of v0, /device:TPU:352, one launch (start us, length us, event | category | flops | bytes accessed | tf_op | source)
XLA Modules:
  0.0 140.1 jit_solution(17545454765826896256)
XLA Ops:
  0.0 2.1 %copy.105 = bf16[128,2048]{0,1:T(8,128)(2,1)} copy(bf16[128,2048]{1,0:T(8,128)(2,1)} %param.13) | data formatting | bytes 1048576 | tf_op args[1]
  2.1 5.3 %all-to-all-start.1 = ((bf16[128,8,256]{0,2,1:T(8,128)(2,1)}), bf16[128,8,256]{0,2,1:T(8,128)(2,1)S(1)}, u32[]{:S(2)}, u32[]{:S(2)}) async-start(bf16[128,8,256]{0,2,1:T(8,128)(2,1)} %bitcast.11), calls=%async_computation.1 | async-start | bytes 1048576 | tf_op jit(solution)/shard_map/all_to_all | solution.py:38
  7.4 2.1 %copy.110 = bf16[128,2048]{0,1:T(8,128)(2,1)} copy(bf16[128,2048]{1,0:T(8,128)(2,1)} %param.14) | data formatting | bytes 1048576 | tf_op args[2]
  9.4 8.0 %all-to-all-done.1 = bf16[128,8,256]{0,2,1:T(8,128)(2,1)S(1)} async-done(((bf16[128,8,256]{0,2,1:T(8,128)(2,1)}), bf16[128,8,256]{0,2,1:T(8,128)(2,1)S(1)}, u32[]{:S(2)}, u32[]{:S(2)}) %all-to-all-start.1) | async-done | bytes 524320 | tf_op jit(solution)/shard_map/all_to_all | solution.py:38
  17.5 3.5 %all-to-all-start.2 = ((bf16[128,8,256]{0,2,1:T(8,128)(2,1)}), bf16[128,8,256]{0,2,1:T(8,128)(2,1)S(1)}, u32[]{:S(2)}, u32[]{:S(2)}) async-start(bf16[128,8,256]{0,2,1:T(8,128)(2,1)} %bitcast.15), calls=%async_computation.2 | async-start | bytes 1048576 | tf_op jit(solution)/shard_map/all_to_all | solution.py:39
  21.0 2.0 %copy.103 = bf16[128,2048]{0,1:T(8,128)(2,1)} copy(bf16[128,2048]{1,0:T(8,128)(2,1)} %param.12) | data formatting | bytes 1048576 | tf_op args[0]
  23.0 8.1 %all-to-all-done.2 = bf16[128,8,256]{0,2,1:T(8,128)(2,1)S(1)} async-done(((bf16[128,8,256]{0,2,1:T(8,128)(2,1)}), bf16[128,8,256]{0,2,1:T(8,128)(2,1)S(1)}, u32[]{:S(2)}, u32[]{:S(2)}) %all-to-all-start.2) | async-done | bytes 524320 | tf_op jit(solution)/shard_map/all_to_all | solution.py:39
  31.1 3.5 %all-to-all-start = ((bf16[128,8,256]{0,2,1:T(8,128)(2,1)}), bf16[128,8,256]{0,2,1:T(8,128)(2,1)S(1)}, u32[]{:S(2)}, u32[]{:S(2)}) async-start(bf16[128,8,256]{0,2,1:T(8,128)(2,1)} %bitcast.9), calls=%async_computation | async-start | bytes 1048576 | tf_op jit(solution)/shard_map/all_to_all | solution.py:37
  35.7 5.0 %collective-permute-start = (bf16[1024,256]{1,0:T(8,128)(2,1)}, bf16[1024,256]{1,0:T(8,128)(2,1)}, u32[]{:S(2)}, u32[]{:S(2)}) collective-permute-start(bf16[1024,256]{1,0:T(8,128)(2,1)} %bitcast.19), channel_id=1, source_target_pairs={{0,32},{32,64},{64,96},{96,128},{128,160},{160,192},{192,224},{224... | collective-permute-start | bytes 1572872 | tf_op jit(solution)/shard_map/ppermute | solution.py:12
  41.8 3.8 %collective-permute-start.1 = (bf16[1024,256]{1,0:T(8,128)(2,1)}, bf16[1024,256]{1,0:T(8,128)(2,1)}, u32[]{:S(2)}, u32[]{:S(2)}) collective-permute-start(bf16[1024,256]{1,0:T(8,128)(2,1)} %bitcast.20), channel_id=1, source_target_pairs={{0,32},{32,64},{64,96},{96,128},{128,160},{160,192},{192,224},{224... | collective-permute-start | bytes 1572872 | tf_op jit(solution)/shard_map/ppermute | solution.py:12
  47.1 1.9 %fusion.55 = (f32[2,1024]{1,0:T(2,128)S(1)}, f32[2,1024,1024]{1,2,0:T(8,128)S(1)}) fusion(pred[1024,1024]{0,1:T(8,128)(4,1)S(1)} %iota_compare_fusion, bf16[1024,2,128]{0,2,1:T(8,128)(2,1)S(1)} %reshape.84, bf16[1024,2,128]{0,2,1:T(8,128)(2,1)S(1)} %reshape.85), kind=kOutput, calls=%fused_computation.54 | convolution fusion | flops 543160320 | bytes 10493952 | tf_op jit(solution)/shard_map/qhd,khd->hqk/dot_general | solution.py:17
  49.0 4.3 %collective-permute-done = bf16[1024,256]{1,0:T(8,128)(2,1)} collective-permute-done((bf16[1024,256]{1,0:T(8,128)(2,1)}, bf16[1024,256]{1,0:T(8,128)(2,1)}, u32[]{:S(2)}, u32[]{:S(2)}) %collective-permute-start) | collective-permute-done | bytes 524320 | tf_op jit(solution)/shard_map/ppermute | solution.py:12
  53.3 5.6 %collective-permute-start.2 = (bf16[1024,256]{1,0:T(8,128)(2,1)}, bf16[1024,256]{1,0:T(8,128)(2,1)}, u32[]{:S(2)}, u32[]{:S(2)}) collective-permute-start(bf16[1024,256]{1,0:T(8,128)(2,1)} %collective-permute-done), channel_id=1, source_target_pairs={{0,32},{32,64},{64,96},{96,128},{128,160},{160,192},{192,224},{224... | collective-permute-start | bytes 1572872 | tf_op jit(solution)/shard_map/ppermute | solution.py:12
  58.9 5.6 %collective-permute-done.1 = bf16[1024,256]{1,0:T(8,128)(2,1)} collective-permute-done((bf16[1024,256]{1,0:T(8,128)(2,1)}, bf16[1024,256]{1,0:T(8,128)(2,1)}, u32[]{:S(2)}, u32[]{:S(2)}) %collective-permute-start.1) | collective-permute-done | bytes 524320 | tf_op jit(solution)/shard_map/ppermute | solution.py:12
  64.6 5.6 %collective-permute-start.3 = (bf16[1024,256]{1,0:T(8,128)(2,1)}, bf16[1024,256]{1,0:T(8,128)(2,1)}, u32[]{:S(2)}, u32[]{:S(2)}) collective-permute-start(bf16[1024,256]{1,0:T(8,128)(2,1)} %collective-permute-done.1), channel_id=1, source_target_pairs={{0,32},{32,64},{64,96},{96,128},{128,160},{160,192},{192,224},{224... | collective-permute-start | bytes 1572872 | tf_op jit(solution)/shard_map/ppermute | solution.py:12
  70.2 2.0 %fusion.57 = f32[2,1024]{1,0:T(2,128)S(1)} fusion(f32[2,1024,1024]{1,2,0:T(8,128)S(1)} %get-tuple-element.194, f32[2,1024]{1,0:T(2,128)S(1)} %get-tuple-element.193, pred[1024,1024]{0,1:T(8,128)(4,1)S(1)} %iota_compare_fusion), kind=kLoop, calls=%fused_computation.56 | loop fusion | flops 8386560 | bytes 9453568 | tf_op jit(solution)/shard_map/reduce_sum | solution.py:23
  72.7 3.0 %collective-permute-done.2 = bf16[1024,256]{1,0:T(8,128)(2,1)} collective-permute-done((bf16[1024,256]{1,0:T(8,128)(2,1)}, bf16[1024,256]{1,0:T(8,128)(2,1)}, u32[]{:S(2)}, u32[]{:S(2)}) %collective-permute-start.2) | collective-permute-done | bytes 524320 | tf_op jit(solution)/shard_map/ppermute | solution.py:12
  75.8 5.6 %collective-permute-start.4 = (bf16[1024,256]{1,0:T(8,128)(2,1)}, bf16[1024,256]{1,0:T(8,128)(2,1)}, u32[]{:S(2)}, u32[]{:S(2)}) collective-permute-start(bf16[1024,256]{1,0:T(8,128)(2,1)} %collective-permute-done.2), channel_id=1, source_target_pairs={{0,32},{32,64},{64,96},{96,128},{128,160},{160,192},{192,224},{224... | collective-permute-start | bytes 1572872 | tf_op jit(solution)/shard_map/ppermute | solution.py:12
  81.4 5.6 %collective-permute-done.3 = bf16[1024,256]{1,0:T(8,128)(2,1)} collective-permute-done((bf16[1024,256]{1,0:T(8,128)(2,1)}, bf16[1024,256]{1,0:T(8,128)(2,1)}, u32[]{:S(2)}, u32[]{:S(2)}) %collective-permute-start.3) | collective-permute-done | bytes 524320 | tf_op jit(solution)/shard_map/ppermute | solution.py:12
  87.0 5.6 %collective-permute-start.5 = (bf16[1024,256]{1,0:T(8,128)(2,1)}, bf16[1024,256]{1,0:T(8,128)(2,1)}, u32[]{:S(2)}, u32[]{:S(2)}) collective-permute-start(bf16[1024,256]{1,0:T(8,128)(2,1)} %collective-permute-done.3), channel_id=1, source_target_pairs={{0,32},{32,64},{64,96},{96,128},{128,160},{160,192},{192,224},{224... | collective-permute-start | bytes 1572872 | tf_op jit(solution)/shard_map/ppermute | solution.py:12
  92.6 5.4 %fusion.64 = f32[1024,2,128]{2,0,1:T(8,128)S(1)} fusion(bf16[1024,2,128]{0,2,1:T(8,128)(2,1)S(1)} %reshape.86, f32[2,1024,1024]{1,2,0:T(8,128)} %copy-done.1, f32[2,1024]{1,0:T(2,128)S(1)} %get-tuple-element.193, pred[1024,1024]{0,1:T(8,128)(4,1)S(1)} %iota_compare_fusion, f32[1024,2]{0,1:T(2,128)S(1)} %get-tuple-element.187), kind=kOutput, calls=%fused_computation.61 | convolution fusion | flops 545521664 | bytes 11026432 | tf_op jit(solution)/shard_map/hqk,khd->qhd/dot_general | solution.py:25
  100.3 5.4 %conditional.3 = ((f32[2,1024]{1,0:T(2,128)S(1)}, f32[2,1024]{1,0:T(2,128)S(1)}, f32[1024,2,128]{2,0,1:T(8,128)S(1)})) conditional(s32[]{:T(128)} %convert_element_type.49, (f32[2,1024]{1,0:T(2,128)S(1)}, f32[2,1024]{1,0:T(2,128)S(1)}, f32[1024,2,128]{2,0,1:T(8,128)S(1)}) %tuple.25, (bf16[1024,2,128]{0,2,1:T(8,128)(2,1)S(1)}, ...), branch_computations={%region_2.3_spmd, %region_3.6_spmd} | conditional | flops 1091049472 | bytes 28966944 | solution.py:74
  103.2 2.5 %fusion.9 = f32[1024,2,128]{2,0,1:T(8,128)S(1)} fusion(f32[2,1024,1024]{1,2,0:T(8,128)S(1)} %get-tuple-element.180, f32[2,1024]{1,0:T(2,128)S(1)} %get-tuple-element.198, f32[1024,2,128]{2,0,1:T(8,128)S(1)} %get-tuple-element.65, bf16[1024,2,128]{2,1,0:T(2,128)(2,1)S(1)} %get-tuple-element.160, f32[1024,2]{0,1:T(2,128)S(1)} %get-tuple-element.173), kind=kOutput, calls=%fused_computation.8 | convolution fusion | flops 543686656 | bytes 11026432 | tf_op jit(solution)/shard_map/cond/branch_1_fun/hqk,khd->qhd/dot_general | solution.py:25
  105.8 7.2 %conditional.4 = ((f32[2,1024]{1,0:T(2,128)S(1)}, f32[2,1024]{1,0:T(2,128)S(1)}, f32[1024,2,128]{2,0,1:T(8,128)S(1)})) conditional(s32[]{:T(128)} %convert_element_type.48, (f32[2,1024]{1,0:T(2,128)S(1)}, f32[2,1024]{1,0:T(2,128)S(1)}, f32[1024,2,128]{2,0,1:T(8,128)S(1)}) %get-tuple-element.211, (bf16[1024,256]{1,0:T(8,128)(2,1)}, ...), branch_computations={%region_6.7_spmd, %region_7.10_spmd} | conditional | flops 1091049472 | bytes 28966944 | solution.py:74
  105.8 2.3 %multiply_reduce_fusion.1 = (f32[2,1024]{1,0:T(2,128)S(1)}, f32[2,1024,1024]{1,2,0:T(8,128)S(1)}) fusion(bf16[1024,2,128]{0,2,1:T(8,128)(2,1)S(1)} %get-tuple-element.162, bf16[1024,256]{1,0:T(8,128)(2,1)} %get-tuple-element.69), kind=kOutput, calls=%fused_computation.17 | convolution fusion | flops 541063168 | bytes 9445376 | tf_op jit(solution)/shard_map/cond/branch_1_fun/qhd,khd->hqk/dot_general | solution.py:17
  109.5 3.5 %fusion.26 = f32[1024,2,128]{2,0,1:T(8,128)S(1)} fusion(f32[2,1024,1024]{1,2,0:T(8,128)S(1)} %get-tuple-element.182, f32[2,1024]{1,0:T(2,128)S(1)} %get-tuple-element.204, f32[1024,2,128]{2,0,1:T(8,128)S(1)} %get-tuple-element.71, f32[1024,2]{0,1:T(2,128)S(1)} %get-tuple-element.175, bf16[1024,256]{1,0:T(8,128)(2,1)} %get-tuple-element.72), kind=kOutput, calls=%fused_computation.24 | convolution fusion | flops 543686656 | bytes 11026432 | tf_op jit(solution)/shard_map/cond/branch_1_fun/hqk,khd->qhd/dot_general | solution.py:25
  113.0 7.3 %conditional.5 = ((f32[2,1024]{1,0:T(2,128)S(1)}, f32[1024,2,128]{2,0,1:T(8,128)S(1)})) conditional(s32[]{:T(128)} %convert_element_type.47, (f32[2,1024]{1,0:T(2,128)S(1)}, f32[1024,2,128]{2,0,1:T(8,128)S(1)}) %tuple.28, (bf16[1024,256]{1,0:T(8,128)(2,1)}, bf16[1024,2,128]{0,2,1:T(8,128)(2,1)S(1)}, f32[2,1024]{1,0:T(2,128)S(1)}, ...), branch_computations={%region_10.11_spmd, %region_11.14_spmd} | conditional | flops 1091049472 | bytes 28950552 | solution.py:74
  113.0 2.4 %multiply_reduce_fusion.2 = (f32[2,1024]{1,0:T(2,128)S(1)}, f32[2,1024,1024]{1,2,0:T(8,128)S(1)}) fusion(bf16[1024,2,128]{0,2,1:T(8,128)(2,1)S(1)} %get-tuple-element.168, bf16[1024,256]{1,0:T(8,128)(2,1)} %get-tuple-element.76), kind=kOutput, calls=%fused_computation.35 | convolution fusion | flops 541063168 | bytes 9445376 | tf_op jit(solution)/shard_map/cond/branch_1_fun/qhd,khd->hqk/dot_general | solution.py:17
  116.8 3.5 %fusion.45 = f32[1024,2,128]{2,0,1:T(8,128)S(1)} fusion(f32[2,1024,1024]{1,2,0:T(8,128)S(1)} %get-tuple-element.184, f32[2,1024]{1,0:T(2,128)S(1)} %get-tuple-element.178, f32[1024,2,128]{2,0,1:T(8,128)S(1)} %get-tuple-element.77, f32[1024,2]{0,1:T(2,128)S(1)} %get-tuple-element.177, bf16[1024,256]{1,0:T(8,128)(2,1)} %get-tuple-element.78), kind=kOutput, calls=%fused_computation.42 | convolution fusion | flops 543686656 | bytes 11026432 | tf_op jit(solution)/shard_map/cond/branch_1_fun/hqk,khd->qhd/dot_general | solution.py:25
  121.9 5.6 %all-to-all-start.3 = ((bf16[8,128,256]{1,2,0:T(8,128)(2,1)}), bf16[8,128,256]{1,2,0:T(8,128)(2,1)S(1)}, u32[]{:S(2)}, u32[]{:S(2)}) async-start(bf16[8,128,256]{1,2,0:T(8,128)(2,1)} %copy.121), calls=%async_computation.3 | async-start | bytes 1048576 | tf_op jit(solution)/shard_map/all_to_all | solution.py:78
  129.0 7.2 %all-to-all-done.3 = bf16[8,128,256]{1,2,0:T(8,128)(2,1)S(1)} async-done(((bf16[8,128,256]{1,2,0:T(8,128)(2,1)}), bf16[8,128,256]{1,2,0:T(8,128)(2,1)S(1)}, u32[]{:S(2)}, u32[]{:S(2)}) %all-to-all-start.3) | async-done | bytes 524320 | tf_op jit(solution)/shard_map/all_to_all | solution.py:78
  136.2 2.9 %fusion.71 = bf16[128,2048]{0,1:T(8,128)(2,1)S(1)} fusion(bf16[1,128,2048]{1,2,0:T(8,128)(2,1)S(1)} %copy.135, bf16[1,128,2048]{1,2,0:T(8,128)(2,1)S(1)} %copy.136, f32[]{:T(128)} %bitcast.25, f32[]{:T(128)} %bitcast.24, f32[]{:T(128)} %bitcast.7, f32[]{:T(128)} %bitcast.6, bf16[8,128,256]{1,2,0:T(8,128)(2,1)S(1)} %all-to-all-done.3), kind=kLoop, calls=%fused_computation.70 | loop fusion | flops 3145728 | bytes 2097168 | tf_op jit(solution)/shard_map/convert_element_type | solution.py:80
  (45 shorter events, 16.0 us)
Async XLA Ops:
  0.0 128.2 %copy-start = (f32[2,64]{1,0:T(2,128)S(1)}, f32[2,64]{1,0:T(2,128)}, u32[]{:S(2)}) copy-start(f32[2,64]{1,0:T(2,128)} %param.17) | copy-start | bytes 1540
  2.1 15.4 %all-to-all-start.1 = ((bf16[128,8,256]{0,2,1:T(8,128)(2,1)}), bf16[128,8,256]{0,2,1:T(8,128)(2,1)S(1)}, u32[]{:S(2)}, u32[]{:S(2)}) async-start(bf16[128,8,256]{0,2,1:T(8,128)(2,1)} %bitcast.11), calls=%async_computation.1 | async-start | bytes 1048576 | tf_op jit(solution)/shard_map/all_to_all | solution.py:38
  17.5 13.7 %all-to-all-start.2 = ((bf16[128,8,256]{0,2,1:T(8,128)(2,1)}), bf16[128,8,256]{0,2,1:T(8,128)(2,1)S(1)}, u32[]{:S(2)}, u32[]{:S(2)}) async-start(bf16[128,8,256]{0,2,1:T(8,128)(2,1)} %bitcast.15), calls=%async_computation.2 | async-start | bytes 1048576 | tf_op jit(solution)/shard_map/all_to_all | solution.py:39
  31.1 14.8 %all-to-all-start = ((bf16[128,8,256]{0,2,1:T(8,128)(2,1)}), bf16[128,8,256]{0,2,1:T(8,128)(2,1)S(1)}, u32[]{:S(2)}, u32[]{:S(2)}) async-start(bf16[128,8,256]{0,2,1:T(8,128)(2,1)} %bitcast.9), calls=%async_computation | async-start | bytes 1048576 | tf_op jit(solution)/shard_map/all_to_all | solution.py:37
  35.7 17.6 %collective-permute-start = (bf16[1024,256]{1,0:T(8,128)(2,1)}, bf16[1024,256]{1,0:T(8,128)(2,1)}, u32[]{:S(2)}, u32[]{:S(2)}) collective-permute-start(bf16[1024,256]{1,0:T(8,128)(2,1)} %bitcast.19), channel_id=1, source_target_pairs={{0,32},{32,64},{64,96},{96,128},{128,160},{160,192},{192,224},{224... | collective-permute-start | bytes 1572872 | tf_op jit(solution)/shard_map/ppermute | solution.py:12
  41.8 22.8 %collective-permute-start.1 = (bf16[1024,256]{1,0:T(8,128)(2,1)}, bf16[1024,256]{1,0:T(8,128)(2,1)}, u32[]{:S(2)}, u32[]{:S(2)}) collective-permute-start(bf16[1024,256]{1,0:T(8,128)(2,1)} %bitcast.20), channel_id=1, source_target_pairs={{0,32},{32,64},{64,96},{96,128},{128,160},{160,192},{192,224},{224... | collective-permute-start | bytes 1572872 | tf_op jit(solution)/shard_map/ppermute | solution.py:12
  49.0 21.1 %copy-start.1 = (f32[2,1024,1024]{1,2,0:T(8,128)}, f32[2,1024,1024]{1,2,0:T(8,128)S(1)}, u32[]{:S(2)}) copy-start(f32[2,1024,1024]{1,2,0:T(8,128)S(1)} %get-tuple-element.194) | copy-start | bytes 25165828
  53.3 22.5 %collective-permute-start.2 = (bf16[1024,256]{1,0:T(8,128)(2,1)}, bf16[1024,256]{1,0:T(8,128)(2,1)}, u32[]{:S(2)}, u32[]{:S(2)}) collective-permute-start(bf16[1024,256]{1,0:T(8,128)(2,1)} %collective-permute-done), channel_id=1, source_target_pairs={{0,32},{32,64},{64,96},{96,128},{128,160},{160,192},{192,224},{224... | collective-permute-start | bytes 1572872 | tf_op jit(solution)/shard_map/ppermute | solution.py:12
  64.6 22.5 %collective-permute-start.3 = (bf16[1024,256]{1,0:T(8,128)(2,1)}, bf16[1024,256]{1,0:T(8,128)(2,1)}, u32[]{:S(2)}, u32[]{:S(2)}) collective-permute-start(bf16[1024,256]{1,0:T(8,128)(2,1)} %collective-permute-done.1), channel_id=1, source_target_pairs={{0,32},{32,64},{64,96},{96,128},{128,160},{160,192},{192,224},{224... | collective-permute-start | bytes 1572872 | tf_op jit(solution)/shard_map/ppermute | solution.py:12
  75.8 37.2 %collective-permute-start.4 = (bf16[1024,256]{1,0:T(8,128)(2,1)}, bf16[1024,256]{1,0:T(8,128)(2,1)}, u32[]{:S(2)}, u32[]{:S(2)}) collective-permute-start(bf16[1024,256]{1,0:T(8,128)(2,1)} %collective-permute-done.2), channel_id=1, source_target_pairs={{0,32},{32,64},{64,96},{96,128},{128,160},{160,192},{192,224},{224... | collective-permute-start | bytes 1572872 | tf_op jit(solution)/shard_map/ppermute | solution.py:12
  87.0 26.0 %collective-permute-start.5 = (bf16[1024,256]{1,0:T(8,128)(2,1)}, bf16[1024,256]{1,0:T(8,128)(2,1)}, u32[]{:S(2)}, u32[]{:S(2)}) collective-permute-start(bf16[1024,256]{1,0:T(8,128)(2,1)} %collective-permute-done.3), channel_id=1, source_target_pairs={{0,32},{32,64},{64,96},{96,128},{128,160},{160,192},{192,224},{224... | collective-permute-start | bytes 1572872 | tf_op jit(solution)/shard_map/ppermute | solution.py:12
  113.0 14.5 %copy-start.2 = (bf16[2,128,2048]{2,1,0:T(8,128)(2,1)S(1)}, bf16[2,128,2048]{2,1,0:T(8,128)(2,1)}, u32[]{:S(2)}) copy-start(bf16[2,128,2048]{2,1,0:T(8,128)(2,1)} %param.15) | copy-start | bytes 3145732
  120.3 7.9 %copy-start.3 = (s32[2]{0:T(128)S(1)}, s32[2]{0:T(128)}, u32[]{:S(2)}) copy-start(s32[2]{0:T(128)} %param.16) | copy-start | bytes 28
  121.9 14.3 %all-to-all-start.3 = ((bf16[8,128,256]{1,2,0:T(8,128)(2,1)}), bf16[8,128,256]{1,2,0:T(8,128)(2,1)S(1)}, u32[]{:S(2)}, u32[]{:S(2)}) async-start(bf16[8,128,256]{1,2,0:T(8,128)(2,1)} %copy.121), calls=%async_computation.3 | async-start | bytes 1048576 | tf_op jit(solution)/shard_map/all_to_all | solution.py:78
where the time goes:
time: 141 us; the launch traced here: 140 us
  starting transfers between devices  49.1 us (35%)
  waiting for transfers between devices  42 us (30%)
  matrix products  22.8 us (16%)
  local copies, waits for them, and re-layouts  15.8 us (11%)
  other arithmetic  9.74 us (7%)
    ppermute x6, starting transfers between devices, from_behind(): return lax.ppermute(block, axis, route)  31.2 us
    ppermute x6, waiting for transfers between devices, from_behind(): return lax.ppermute(block, axis, route)  18.6 us
    dot_general x4, matrix products, block_update(): jnp.einsum('hqk,khd->qhd', weights, value_heads, preferred_element_type=j...  14.8 us
    all_to_all x1, waiting for transfers between devices, shards(): lax.all_to_all(values, 'uly', split_axis=1, concat_axis=0, tiled=True)  8.14 us
    all_to_all x1, waiting for transfers between devices, shards(): lax.all_to_all(keys, 'uly', split_axis=1, concat_axis=0, tiled=True)  8.03 us
    dot_general x4, matrix products, block_update(): jnp.einsum('qhd,khd->hqk', query_heads, key_heads, preferred_element_type...  7.87 us
    all_to_all x1, waiting for transfers between devices, shards(): lax.all_to_all(attended, 'uly', split_axis=0, concat_axis=1, tiled=True)  7.17 us
    unnamed x14, local copies, waits for them, and re-layouts  6.82 us
  transfers between devices with their start and end apart: 10, of which 7 were waited for; matrix products, arithmetic and copies ran while one was open for 24% of the time, Pallas kernels for 0%

commit v1 on v0

v1 whole, which is shorter than its diff:
```python
import functools
import math

import jax
import jax.numpy as jnp
from jax import lax
from jax.experimental import pallas as pl
from jax.experimental.pallas import tpu as pltpu
from jax.sharding import PartitionSpec as P

MESH = pl.DeviceIdType.MESH
HEAD_DIM = 128
SCALE = math.log2(math.e) / math.sqrt(HEAD_DIM)
BF16, F32 = jnp.bfloat16, jnp.float32

PLACES = ((0, 0), (0, 1), (0, 3), (1, 0), (1, 1), (1, 3), (0, 2), (1, 2))
MIRROR = tuple(PLACES.index((dy, (4 - dx) % 4)) for dy, dx in PLACES)

ORDER = (
    ("S0", 0), ("S0", 1), ("S0", 2), ("R1", 0), ("R1", 1), ("C1", 0), ("R1", 2), ("C1", 1), ("C1", 2), ("C0", 0),
    ("R2", 0), ("C2", 0), ("C0", 1), ("R2", 1), ("C2", 1), ("C0", 2), ("R2", 2), ("C2", 2), ("C0", 3), ("C3", 0),
    ("S0", 3), ("C3", 1), ("S0", 4), ("C0", 4), ("C3", 2), ("S0", 5), ("C0", 5), ("M2", 0), ("C0", 6), ("R1", 3),
    ("C1", 3), ("M2", 1), ("C0", 7), ("R1", 4), ("C1", 4), ("M2", 2), ("R1", 5), ("C1", 5), ("M1", 0), ("R2", 3),
    ("C2", 3), ("M1", 1), ("R2", 4), ("C2", 4), ("M1", 2), ("R2", 5), ("C2", 5), ("M0", 0), ("C3", 3), ("M0", 1),
    ("S0", 6), ("C3", 4), ("M0", 2), ("S0", 7), ("C3", 5), ("M2", 3), ("R1", 6), ("C1", 6), ("M2", 4), ("R1", 7),
    ("C1", 7), ("M2", 5), ("R2", 6), ("C2", 6), ("M1", 3), ("R2", 7), ("C2", 7), ("M1", 4), ("M1", 5), ("M0", 3),
    ("C3", 6), ("M0", 4), ("C3", 7), ("M0", 5), ("M2", 6), ("M2", 7), ("M1", 6), ("M1", 7), ("M0", 6), ("M0", 7),
)


def kernel(
    q_hbm, k_hbm, v_hbm, out,
    qb, kb, vb, vt, q1, q2, q3, o_in, l_in, o_out, l_out, acc, top, tot, scores, ready,
    ex_send, ex_recv, q_send, q_recv, o_send, l_send, o_recv, l_recv, f_send, f_recv,
):
    z = lax.axis_index("seq")
    n_z = lax.axis_size("seq")
    me = lax.axis_index("uly")
    y, x = me // 4, lax.rem(me, 4)

    def peer(place):
        dy, dx = PLACES[place]
        return lax.rem(y + dy, 2) * 4 + lax.rem(x + dx, 4)

    below, above = z > 0, z < n_z - 1
    barrier = pltpu.get_barrier_semaphore()
    for p in range(1, 8):
        pl.semaphore_signal(barrier, inc=1, device_id={"uly": peer(p)}, device_id_type=MESH)

    @pl.when(below)
    def _():
        pl.semaphore_signal(barrier, inc=1, device_id={"seq": z - 1}, device_id_type=MESH)

    @pl.when(above)
    def _():
        pl.semaphore_signal(barrier, inc=1, device_id={"seq": z + 1}, device_id_type=MESH)

    gathered = ((q_hbm, qb), (k_hbm, kb), (v_hbm, vb))

    def own_copy(t, h):
        src, dst = gathered[t]
        columns = pl.ds(pl.multiple_of((me * 2 + h) * HEAD_DIM, HEAD_DIM), HEAD_DIM)
        return pltpu.make_async_copy(src.at[:, columns], dst.at[h, pl.ds(0, 128)], ex_recv.at[t, h, 0])

    def exchange(t, h, p):
        src, dst = gathered[t]
        to = peer(MIRROR[p])
        columns = pl.ds(pl.multiple_of((to * 2 + h) * HEAD_DIM, HEAD_DIM), HEAD_DIM)
        return pltpu.make_async_remote_copy(
            src_ref=src.at[:, columns], dst_ref=dst.at[h, pl.ds(p * 128, 128)],
            send_sem=ex_send.at[t], recv_sem=ex_recv.at[t, h, p], device_id={"uly": to}, device_id_type=MESH,
        )

    for h in range(2):
        for t in range(3):
            own_copy(t, h).start()

    @pl.when(z == 0)
    def _():
        o_in[...] = jnp.zeros_like(o_in)
        l_in[...] = jnp.full_like(l_in, -1e30)

    pl.semaphore_wait(barrier, 7 + jnp.where(below, 1, 0) + jnp.where(above, 1, 0))

    for h in range(2):
        for t in range(3):
            for p in range(1, 8):
                exchange(t, h, p).start()

    blocks = (qb, q1, q2, q3)

    def rows_of(chunk):
        return chunk // 4, pl.ds((chunk % 4) * 256, 256)

    def down(level, chunk):
        h, rows = rows_of(chunk)
        return pltpu.make_async_remote_copy(
            src_ref=blocks[level].at[h, rows], dst_ref=blocks[level + 1].at[h, rows],
            send_sem=q_send.at[level], recv_sem=q_recv.at[level, chunk],
            device_id={"seq": jnp.maximum(z - 1, 0)}, device_id_type=MESH,
        )

    def up(level, chunk):
        to = jnp.minimum(z + 1, n_z - 1)
        return [
            pltpu.make_async_remote_copy(
                src_ref=src.at[level, chunk], dst_ref=dst.at[level, chunk],
                send_sem=send.at[level], recv_sem=recv.at[level, chunk], device_id={"seq": to}, device_id_type=MESH,
            )
            for src, dst, send, recv in ((o_out, o_in, o_send, o_recv), (l_out, l_in, l_send, l_recv))
        ]

    def finish(chunk, i):
        h, place = chunk // 4, (chunk % 4) * 2 + i
        columns = pl.ds(pl.multiple_of((me * 2 + h) * HEAD_DIM, HEAD_DIM), HEAD_DIM)
        return pltpu.make_async_remote_copy(
            src_ref=ready.at[h, pl.ds(place * 128, 128)], dst_ref=out.at[:, columns],
            send_sem=f_send, recv_sem=f_recv.at[h, MIRROR[place]], device_id={"uly": peer(place)}, device_id_type=MESH,
        )

    def attend(level, chunk):
        h, rows = rows_of(chunk)
        query = blocks[level][h, rows]
        nt = (((1,), (1,)), ((), ()))
        tops = []
        for b in range(4):
            s = lax.dot_general(kb[h, pl.ds(b * 256, 256)], query, nt, preferred_element_type=F32)
            if level == 0:
                key_row = lax.broadcasted_iota(jnp.int32, (256, 1), 0)
                query_row = lax.broadcasted_iota(jnp.int32, (1, 256), 1)
                key_pos = jnp.where(key_row < 128, peer(2 * b) * 128, peer(2 * b + 1) * 128 - 128) + key_row
                first = 2 * (chunk % 4)
                query_pos = jnp.where(query_row < 128, peer(first) * 128, peer(first + 1) * 128 - 128) + query_row
                s = jnp.where(key_pos <= query_pos, s, -1e30)
            scores[pl.ds(b * 256, 256)] = s
            tops.append(jnp.max(s, axis=0, keepdims=True))
        top_ = jnp.maximum(jnp.maximum(tops[0], tops[1]), jnp.maximum(tops[2], tops[3]))
        total = jnp.zeros((1, 256), F32)
        weighted = jnp.zeros((128, 256), F32)
        for b in range(4):
            prob = jnp.exp2((scores[pl.ds(b * 256, 256)] - top_) * SCALE)
            total += jnp.sum(prob, axis=0, keepdims=True)
            weighted += lax.dot_general(
                vt[h, :, pl.ds(b * 256, 256)], prob.astype(BF16), (((1,), (0,)), ((), ())), preferred_element_type=F32
            )
        return weighted, top_ * SCALE, total

    def merged(level, chunk):
        new = l_in[level, chunk]
        own = top[level, chunk]
        most = jnp.maximum(own, new)
        a, b = jnp.exp2(own - most), jnp.exp2(new - most)
        total = tot[level, chunk] * a + b
        weighted = acc[level, chunk] * a + o_in[level, chunk].astype(F32) * b
        return weighted / total, most + jnp.log2(total)

    waited = set()

    def head_ready(h):
        if h in waited:
            return
        waited.add(h)
        for t in (1, 2):
            own_copy(t, h).wait()
            for p in range(1, 8):
                exchange(t, h, p).wait_recv()
        vt[h] = jnp.transpose(vb[h])

    def own_queries(chunk):
        for i in range(2):
            h, p = chunk // 4, (chunk % 4) * 2 + i
            if ("q", h, p) in waited:
                continue
            waited.add(("q", h, p))
            if p == 0:
                own_copy(0, h).wait()
            else:
                exchange(0, h, p).wait_recv()

    def has(level):
        return z < n_z - level

    for step, chunk in ORDER:
        h, rows = rows_of(chunk)
        level = int(step[1])
        if step == "S0":
            own_queries(chunk)

            @pl.when(below)
            def _(chunk=chunk):
                down(0, chunk).start()
        elif step[0] == "R":

            @pl.when(has(level))
            def _(chunk=chunk, level=level):
                down(level - 1, chunk).wait_recv()

            @pl.when(has(level) & below)
            def _(chunk=chunk, level=level):
                down(level, chunk).start()
        elif step == "C3":
            head_ready(h)

            @pl.when(has(3))
            def _(chunk=chunk):
                down(2, chunk).wait_recv()
                weighted, top_, total = attend(3, chunk)
                o_out[2, chunk] = (weighted / total).astype(BF16)
                l_out[2, chunk] = top_ + jnp.log2(total)
                for copy in up(2, chunk):
                    copy.start()
        elif step[0] == "C":
            head_ready(h)
            if level == 0:
                own_queries(chunk)

            @pl.when(has(level))
            def _(chunk=chunk, level=level):
                weighted, top_, total = attend(level, chunk)
                acc[level, chunk] = weighted
                top[level, chunk] = top_
                tot[level, chunk] = total
        elif step == "M0":

            @pl.when(below)
            def _(chunk=chunk):
                for copy in up(0, chunk):
                    copy.wait_recv()

            mean, _unused = merged(0, chunk)
            ready[h, rows] = jnp.transpose(mean).astype(BF16)
            for i in range(2):
                if (chunk % 4) * 2 + i == 0:
                    columns = pl.ds(pl.multiple_of((me * 2 + h) * HEAD_DIM, HEAD_DIM), HEAD_DIM)
                    out[:, columns] = ready[h, pl.ds(0, 128)]
                else:
                    finish(chunk, i).start()
        else:

            @pl.when(has(level) & below)
            def _(chunk=chunk, level=level):
                for copy in up(level, chunk):
                    copy.wait_recv()

            @pl.when(has(level))
            def _(chunk=chunk, level=level):
                mean, log_total = merged(level, chunk)
                o_out[level - 1, chunk] = mean.astype(BF16)
                l_out[level - 1, chunk] = log_total
                for copy in up(level - 1, chunk):
                    copy.start()

    for h in range(2):
        for place in range(1, 8):
            src = pl.ds(pl.multiple_of((peer(place) * 2 + h) * HEAD_DIM, HEAD_DIM), HEAD_DIM)
            pltpu.make_async_remote_copy(
                src_ref=ready.at[h, pl.ds(0, 128)], dst_ref=out.at[:, src],
                send_sem=f_send, recv_sem=f_recv.at[h, place], device_id={"uly": peer(place)}, device_id_type=MESH,
            ).wait_recv()

    for t, (_src, dst) in enumerate(gathered):
        sent = dst.at[:, pl.ds(0, 896)]
        pltpu.make_async_copy(sent, sent, ex_send.at[t]).wait()
    sent = ready.at[:, pl.ds(0, 896)]
    pltpu.make_async_copy(sent, sent, f_send).wait()
    for level in range(3):

        @pl.when(has(level) & below)
        def _(level=level):
            sent = blocks[level]
            pltpu.make_async_copy(sent, sent, q_send.at[level]).wait()

        @pl.when(has(level + 1))
        def _(level=level):
            for src, sem in ((o_out, o_send), (l_out, l_send)):
                sent = src.at[level]
                pltpu.make_async_copy(sent, sent, sem.at[level]).wait()


def attention(queries, keys, values):
    block = pltpu.VMEM((2, 1024, HEAD_DIM), BF16)
    dma = pltpu.SemaphoreType.DMA
    hbm = pl.BlockSpec(memory_space=pl.ANY)
    return pl.pallas_call(
        kernel,
        out_shape=jax.ShapeDtypeStruct(queries.shape, BF16),
        in_specs=[hbm, hbm, hbm],
        out_specs=pl.BlockSpec(memory_space=pltpu.VMEM),
        scratch_shapes=[
            block, block, block, pltpu.VMEM((2, HEAD_DIM, 1024), BF16), block, block, block,
            pltpu.VMEM((3, 8, HEAD_DIM, 256), BF16), pltpu.VMEM((3, 8, 1, 256), F32),
            pltpu.VMEM((3, 8, HEAD_DIM, 256), BF16), pltpu.VMEM((3, 8, 1, 256), F32),
            pltpu.VMEM((3, 8, HEAD_DIM, 256), F32), pltpu.VMEM((3, 8, 1, 256), F32), pltpu.VMEM((3, 8, 1, 256), F32),
            pltpu.VMEM((1024, 256), F32), block,
            dma((3,)), dma((3, 2, 8)), dma((3,)), dma((3, 8)), dma((3,)), dma((3,)), dma((3, 8)), dma((3, 8)),
            dma(()), dma((2, 8)),
        ],
        compiler_params=pltpu.CompilerParams(collective_id=0, has_side_effects=True),
        name="attention",
    )(queries, keys, values)


def shards(queries, keys, values, past_outputs, dwa_slot, dwa_table):
    attended = attention(queries, keys, values)
    onehot = (dwa_slot[:, None] == jnp.arange(dwa_table.shape[1])[None, :]).astype(F32)
    coefs = jnp.dot(onehot, jnp.transpose(dwa_table), precision=lax.Precision.HIGHEST)
    layer_in = jnp.zeros(queries.shape, F32)
    extra = jnp.zeros(queries.shape, F32)
    for index in range(past_outputs.shape[0]):
        stored = past_outputs[index].astype(F32)
        layer_in = layer_in + coefs[index, 0] * stored
        extra = extra + coefs[index, 1] * stored
    hidden = layer_in + attended.astype(F32)
    return (hidden + extra).astype(BF16)


def solution(mesh):
    tokens = P(("rep", "seq", "uly"), None)
    return jax.shard_map(
        shards,
        mesh=mesh,
        in_specs=(tokens, tokens, tokens, P(None, ("rep", "seq", "uly"), None), P(), P()),
        out_specs=tokens,
        check_vma=False,
    )
```

time: 141 us -> 80.5 us (0.57)
  the two profiles are of different devices: /device:TPU:352 before, /device:TPU:704 now
where the time goes in v1:
time: 80.5 us; the launch traced here: 80.2 us
  Pallas kernels  73.2 us (91%)
  other arithmetic  4.78 us (6%)
  local copies, waits for them, and re-layouts  1.35 us (2%)
  matrix products  0.84 us (1%)
    pallas_call x1, Pallas kernels, attention(): pl.pallas_call(kernel, out_shape=jax.ShapeDtypeStruct(queries.shape, BF16...  73.2 us
    convert_element_type x1, other arithmetic, shards(): return (hidden + extra).astype(BF16)  4.78 us

profile of v1, /device:TPU:704, one launch (start us, length us, event | category | flops | bytes accessed | tf_op | source)
XLA Modules:
  0.0 80.2 jit_solution(8458852762033079825)
XLA Ops:
  0.0 0.0 copy-start
  0.0 0.7 copy-done
  0.7 0.8 %fusion.7 = f32[2,2]{1,0:T(2,128)S(1)} fusion(f32[2,64]{1,0:T(2,128)S(1)} %copy-done, s32[2]{0:T(128)} %param.10), kind=kOutput, calls=%fused_computation.11 | convolution fusion | flops 3200 | bytes 536 | tf_op jit(solution)/shard_map/dot_general | solution.py:306
  1.5 0.7 fusion.11
  2.2 0.0 copy-start.1
  2.2 73.2 %attention.1 = bf16[128,2048]{1,0:T(8,128)(2,1)} custom-call(bf16[128,2048]{1,0:T(8,128)(2,1)} %q_hbm.1, bf16[128,2048]{1,0:T(8,128)(2,1)} %k_hbm.1, bf16[128,2048]{1,0:T(8,128)(2,1)} %v_hbm.1), custom_call_target="tpu_custom_call" | custom-call | tf_op jit(solution)/shard_map/attention/pallas_call | solution.py:284
  75.4 0.0 copy-done.1
  75.4 4.8 %fusion.4 = bf16[128,2048]{1,0:T(8,128)(2,1)} fusion(bf16[128,2048]{1,0:T(8,128)(2,1)} %attention.1, f32[]{:T(128)} %bitcast.4, f32[]{:T(128)} %bitcast.3, bf16[2,128,2048]{2,1,0:T(8,128)(2,1)S(1)} %copy-done.1, f32[]{:T(128)} %bitcast.1, f32[]{:T(128)} %bitcast), kind=kLoop, calls=%fused_computation.8 | loop fusion | flops 3145728 | bytes 2097168 | tf_op jit(solution)/shard_map/convert_element_type | solution.py:314
Async XLA Ops:
  0.0 0.7 copy-start
  2.2 73.2 %copy-start.1 = (bf16[2,128,2048]{2,1,0:T(8,128)(2,1)S(1)}, bf16[2,128,2048]{2,1,0:T(8,128)(2,1)}, u32[]{:S(2)}) copy-start(bf16[2,128,2048]{2,1,0:T(8,128)(2,1)} %param.9) | copy-start | bytes 3145732

commit v2 on v0

v2 whole, which is shorter than its diff:
```python
import functools
import math

import jax
import jax.numpy as jnp
from jax import lax
from jax.experimental import pallas as pl
from jax.experimental.pallas import tpu as pltpu
from jax.sharding import PartitionSpec as P

MESH = pl.DeviceIdType.MESH
HEAD_DIM = 128
SCALE = math.log2(math.e) / math.sqrt(HEAD_DIM)
BF16, F32 = jnp.bfloat16, jnp.float32
NT = (((1,), (1,)), ((), ()))
NN = (((1,), (0,)), ((), ()))

PLACES = ((0, 0), (0, 1), (0, 3), (1, 0), (1, 1), (1, 3), (0, 2), (1, 2))
MIRROR = tuple(PLACES.index((dy, (4 - dx) % 4)) for dy, dx in PLACES)

MODES = ((1, 2), (0, 3))
EXCHANGE = ((0, 0, 0, 4), (1, 0, 0, 8), (2, 0, 0, 8), (0, 0, 4, 8), (1, 1, 0, 8), (2, 1, 0, 8), (0, 1, 0, 8))

STEPS = ("S0", "R1", "R2", "C3", "C2", "C1", "C0", "M2", "M1", "M0", "KV", "KF", "SK", "SV")
ORDER = (
    208, 192, 8, 1, 2, 193, 0, 3, 194, 196, 24, 195, 17, 198, 211, 16, 19, 199, 210, 18, 209, 212, 197, 4,
    160, 5, 6, 215, 64, 7, 214, 96, 213, 40, 20, 65, 21, 99, 22, 81, 80, 23, 176, 49, 9, 114, 115, 10,
    48, 11, 50, 113, 112, 12, 66, 13, 117, 161, 25, 116, 67, 131, 26, 130, 51, 27, 14, 15, 82, 118, 129, 119,
    133, 41, 42, 132, 68, 43, 28, 83, 84, 101, 29, 30, 134, 135, 52, 69, 31, 53, 44, 45, 97, 120, 46, 98,
    47, 121, 85, 122, 151, 150, 123, 54, 55, 138, 100, 148, 87, 70, 86, 124, 71, 125, 146, 126, 127, 139, 141, 145,
    142, 143, 154, 140, 137, 102, 149, 103, 158, 157, 128, 155, 159, 147, 156, 153, 136, 144, 152,
)


def kernel(
    slot, table, q_hbm, k_hbm, v_hbm, past_hbm, out,
    qb, kb, vb, vt, q1, q2, q3, kf, vf, vft, o_in, l_in, o_out, l_out, acc, top, tot, scores, ready, past, base, came,
    ex_send, ex_recv, q_send, q_recv, kv_send, kv_recv, o_send, l_send, o_recv, l_recv, f_send, f_recv, past_sem,
):
    z = lax.axis_index("seq")
    n_z = lax.axis_size("seq")
    me = lax.axis_index("uly")
    y, x = me // 4, lax.rem(me, 4)
    below, above = z > 0, z < n_z - 1
    to_lower = {"seq": jnp.maximum(z - 1, 0)}
    to_upper = {"seq": jnp.minimum(z + 1, n_z - 1)}

    def peer(place):
        dy, dx = PLACES[place]
        return lax.rem(y + dy, 2) * 4 + lax.rem(x + dx, 4)

    def has(level):
        return z < n_z - level

    def columns_of(device, h):
        return pl.ds(pl.multiple_of((device * 2 + h) * HEAD_DIM, HEAD_DIM), HEAD_DIM)

    def place_rows(p):
        return pl.ds(p * 128, 128)

    barrier = pltpu.get_barrier_semaphore()
    for p in range(1, 8):
        pl.semaphore_signal(barrier, inc=1, device_id={"uly": peer(p)}, device_id_type=MESH)

    @pl.when(below)
    def _():
        pl.semaphore_signal(barrier, inc=1, device_id=to_lower, device_id_type=MESH)

    @pl.when(above)
    def _():
        pl.semaphore_signal(barrier, inc=1, device_id=to_upper, device_id_type=MESH)

    gathered = ((q_hbm, qb), (k_hbm, kb), (v_hbm, vb))

    def own_copy(t, h):
        src, dst = gathered[t]
        return pltpu.make_async_copy(src.at[:, columns_of(me, h)], dst.at[h, place_rows(0)], ex_recv.at[t, h, 0])

    def exchange(t, h, p):
        src, dst = gathered[t]
        to = peer(MIRROR[p])
        return pltpu.make_async_remote_copy(
            src_ref=src.at[:, columns_of(to, h)], dst_ref=dst.at[h, place_rows(p)],
            send_sem=ex_send.at[t], recv_sem=ex_recv.at[t, h, p], device_id={"uly": to}, device_id_type=MESH,
        )

    for h in range(2):
        for t in range(3):
            own_copy(t, h).start()
    past_copy = pltpu.make_async_copy(past_hbm, past, past_sem)
    past_copy.start()

    @pl.when(z == 0)
    def _():
        o_in[...] = jnp.zeros_like(o_in)
        l_in[...] = jnp.full_like(l_in, -1e30)
        kf[...] = jnp.zeros_like(kf)
        vf[...] = jnp.zeros_like(vf)

    past_copy.wait()
    coefs = [table[0, slot[i]] + table[1, slot[i]] for i in range(2)]

    def stored_sum(i, carry):
        rows = pl.ds(pl.multiple_of(i * 16, 16), 16)
        base[rows] = past[0, rows].astype(F32) * coefs[0] + past[1, rows].astype(F32) * coefs[1]
        return carry

    lax.fori_loop(0, 8, stored_sum, 0)

    pl.semaphore_wait(barrier, 7 + jnp.where(below, 1, 0) + jnp.where(above, 1, 0))

    for t, h, first, last in EXCHANGE:
        for p in range(max(first, 1), last):
            exchange(t, h, p).start()

    blocks = (qb, q1, q2, q3)

    def split(chunk):
        return chunk // 8, place_rows(chunk % 8)

    def down(level, chunk):
        h, rows = split(chunk)
        return pltpu.make_async_remote_copy(
            src_ref=blocks[level].at[h, rows], dst_ref=blocks[level + 1].at[h, rows],
            send_sem=q_send.at[level, h], recv_sem=q_recv.at[level, chunk], device_id=to_lower, device_id_type=MESH,
        )

    def forward(t, chunk):
        h, rows = split(chunk)
        src, dst = ((kb, kf), (vb, vf))[t]
        return pltpu.make_async_remote_copy(
            src_ref=src.at[h, rows], dst_ref=dst.at[h, rows],
            send_sem=kv_send.at[t, h], recv_sem=kv_recv.at[t, chunk], device_id=to_upper, device_id_type=MESH,
        )

    def up(level, chunk):
        h = chunk // 8
        return [
            pltpu.make_async_remote_copy(
                src_ref=src.at[level, chunk], dst_ref=dst.at[level, chunk],
                send_sem=send.at[level, h], recv_sem=recv.at[level, chunk], device_id=to_upper, device_id_type=MESH,
            )
            for src, dst, send, recv in ((o_out, o_in, o_send, o_recv), (l_out, l_in, l_send, l_recv))
        ]

    def finish(chunk):
        h, rows = split(chunk)
        place = chunk % 8
        return pltpu.make_async_remote_copy(
            src_ref=ready.at[h, rows], dst_ref=came.at[MIRROR[place], h], send_sem=f_send,
            recv_sem=f_recv.at[MIRROR[place], h], device_id={"uly": peer(place)}, device_id_type=MESH,
        )

    done = set()

    def expect(*wanted):
        by_condition = {}
        for condition, key, copies in wanted:
            if key not in done:
                done.add(key)
                by_condition.setdefault(id(condition), (condition, []))[1].extend(copies)
        for condition, copies in by_condition.values():

            def wait(copies=copies):
                for copy in copies:
                    copy()

            if condition is None:
                wait()
            else:
                pl.when(condition)(wait)

    exists = [None, has(1), has(2), has(3)]
    came_up = [below, has(1) & below, has(2) & below]

    def gathered_rows(t, h, p):
        copy = own_copy(t, h).wait if p == 0 else exchange(t, h, p).wait_recv
        return (None, ("gathered", t, h, p), [copy])

    def queries(level, chunk):
        if level == 0:
            return gathered_rows(0, chunk // 8, chunk % 8)
        return (exists[level], ("down", level, chunk), [down(level - 1, chunk).wait_recv])

    def part(level, chunk):
        return (came_up[level], ("up", level, chunk), [copy.wait_recv for copy in up(level, chunk)])

    def first_stage(step, pair, buffer):
        level = int(step[1])
        h, rows = pair // 4, pl.ds((pair % 4) * 256, 256)
        keys = kb
        source = blocks[level]
        if level == 3 and MODES[h][0] == 1:
            keys, source = kf, q2
        query = source[h, rows]
        tops = []
        for b in range(4):
            s = lax.dot_general(keys[h, pl.ds(b * 256, 256)], query, NT, preferred_element_type=F32)
            if level == 0:
                key_row = lax.broadcasted_iota(jnp.int32, (256, 1), 0)
                query_row = lax.broadcasted_iota(jnp.int32, (1, 256), 1)
                key_pos = jnp.where(key_row < 128, peer(2 * b) * 128, peer(2 * b + 1) * 128 - 128) + key_row
                first = 2 * (pair % 4)
                query_pos = jnp.where(query_row < 128, peer(first) * 128, peer(first + 1) * 128 - 128) + query_row
                s = jnp.where(key_pos <= query_pos, s, -1e30)
            scores[buffer, pl.ds(b * 256, 256)] = s
            tops.append(jnp.max(s.reshape(32, 8, 256), axis=0))
        tops = jnp.maximum(jnp.maximum(tops[0], tops[1]), jnp.maximum(tops[2], tops[3]))
        return jnp.max(tops, axis=0, keepdims=True)

    def second_stage(step, pair, buffer, highest):
        level = int(step[1])
        h = pair // 4
        values = vft if level == 3 and MODES[h][0] == 1 else vt
        total = jnp.zeros((8, 256), F32)
        weighted = None
        for b in range(4):
            prob = jnp.exp2((scores[buffer, pl.ds(b * 256, 256)] - highest) * SCALE)
            total += jnp.sum(prob.reshape(32, 8, 256), axis=0)
            term = lax.dot_general(
                values[h, :, pl.ds(b * 256, 256)], prob.astype(BF16), NN, preferred_element_type=F32
            )
            weighted = term if weighted is None else weighted + term
        return weighted, jnp.sum(total, axis=0, keepdims=True)

    pending = []
    turn = [0]

    def advance(step=None, pair=None):
        last = pending.pop() if pending else None
        if step is not None:
            buffer = turn[0] % 2
            turn[0] += 1
            level = int(step[1])
            highest = first_stage(step, pair, buffer)
        if last is not None:
            old_step, old_pair, old_buffer = last
            old = int(old_step[1])
            old_top = top[old, old_pair]
            weighted, total = second_stage(old_step, old_pair, old_buffer, old_top)
            if old == 3 and MODES[old_pair // 4][1] == 3:
                mean = (weighted / total).astype(BF16)
                log_total = old_top * SCALE + jnp.log2(total)
                for i in range(2):
                    o_out[2, 2 * old_pair + i] = mean[:, i * 128 : i * 128 + 128]
                    l_out[2, 2 * old_pair + i] = log_total[:, i * 128 : i * 128 + 128]
            else:
                acc[old, old_pair] = weighted
                tot[old, old_pair] = total
                if old == 3:
                    top[old, old_pair] = jnp.where(below, old_top, -1e30)
        if step is not None:
            top[level, pair] = highest
            pending.append((step, pair, buffer))
        if last is not None and old == 3 and MODES[old_pair // 4][1] == 3:

            @pl.when(has(3))
            def _():
                for i in range(2):
                    for copy in up(2, 2 * old_pair + i):
                        copy.start()

    def settle(*units):
        if pending and pending[0][:2] in units:
            advance()

    def merged(chunk, level):
        pair, lanes = chunk // 2, slice(chunk % 2 * 128, chunk % 2 * 128 + 128)
        own = top[level, pair][:, lanes] * SCALE
        if level == 2 and MODES[chunk // 8][0] == 1:
            new = top[3, pair][:, lanes] * SCALE
            new_total, new_weighted = tot[3, pair][:, lanes], acc[3, pair, :, lanes]
        else:
            new = l_in[level, chunk]
            new_total, new_weighted = 1.0, o_in[level, chunk].astype(F32)
        most = jnp.maximum(own, new)
        a, b = jnp.exp2(own - most), jnp.exp2(new - most)
        total = tot[level, pair][:, lanes] * a + new_total * b
        weighted = acc[level, pair, :, lanes] * a + new_weighted * b
        return weighted / total, most + jnp.log2(total)

    for code in ORDER:
        step, which = STEPS[code // 16], code % 16
        if step in ("S0", "R1", "R2"):
            level = STEPS.index(step)
            expect(queries(level, which))
            pl.when(has(level) & below)(down(level, which).start)
        elif step in ("SK", "SV"):
            t = STEPS.index(step) - STEPS.index("SK")
            expect(gathered_rows(t + 1, which // 8, which % 8))
            pl.when(above)(forward(t, which).start)
        elif step == "KV":
            expect(*(gathered_rows(t, which, p) for t in (1, 2) for p in range(8)))
            vt[which] = jnp.transpose(vb[which])
        elif step == "KF":
            chunks = range(which * 8, which * 8 + 8)
            expect(*((below, ("kf", t, c), [forward(t, c).wait_recv]) for t in (0, 1) for c in chunks))
            vft[which] = jnp.transpose(vf[which])
        elif step[0] == "C":
            level = int(step[1])
            if level == 3 and MODES[which // 4][0] == 1:
                level = 2
            expect(queries(level, 2 * which), queries(level, 2 * which + 1))
            advance(step, which)
        elif step == "M0":
            settle(("C0", which // 2))
            expect(part(0, which))
            mean, _unused = merged(which, 0)
            h, rows = split(which)
            if which % 8 == 0:
                came[0, h] = jnp.transpose(mean).astype(BF16)
            else:
                ready[h, rows] = jnp.transpose(mean).astype(BF16)
                finish(which).start()
        else:
            level = int(step[1])
            if level == 2 and MODES[which // 8][0] == 1:
                settle(("C2", which // 2), ("C3", which // 2))
            else:
                settle((f"C{level}", which // 2))
                expect(part(level, which))
            mean, log_total = merged(which, level)
            o_out[level - 1, which] = mean.astype(BF16)
            l_out[level - 1, which] = log_total

            @pl.when(has(level))
            def _(level=level, which=which):
                for copy in up(level - 1, which):
                    copy.start()

    for code in ORDER:
        step, which = STEPS[code // 16], code % 16
        if step == "M0":
            h, place = which // 8, MIRROR[which % 8]
            if place:
                pltpu.make_async_remote_copy(
                    src_ref=ready.at[h, place_rows(place)], dst_ref=came.at[place, h], send_sem=f_send,
                    recv_sem=f_recv.at[place, h], device_id={"uly": peer(place)}, device_id_type=MESH,
                ).wait_recv()
            lanes = columns_of(peer(place), h)
            out[:, lanes] = (base[:, lanes] + came[place, h].astype(F32)).astype(BF16)

    for t, (_src, dst) in enumerate(gathered):
        sent = dst.at[:, pl.ds(0, 896)]
        pltpu.make_async_copy(sent, sent, ex_send.at[t]).wait()
    sent = ready.at[:, pl.ds(0, 896)]
    pltpu.make_async_copy(sent, sent, f_send).wait()

    def all_left(condition, sent, sem):
        pl.when(condition)(pltpu.make_async_copy(sent, sent, sem).wait)

    for h, (up_hops, down_hops) in enumerate(MODES):
        chunks = pl.ds(h * 8, 8)
        for level in range(down_hops):
            all_left(has(level) & below, blocks[level].at[h], q_send.at[level, h])
            all_left(has(level + 1), o_out.at[level, chunks], o_send.at[level, h])
            all_left(has(level + 1), l_out.at[level, chunks], l_send.at[level, h])
        if up_hops:
            all_left(above, kb.at[h], kv_send.at[0, h])
            all_left(above, vb.at[h], kv_send.at[1, h])


def attention(slot, table, queries, keys, values, past):
    block = pltpu.VMEM((2, 1024, HEAD_DIM), BF16)
    turned = pltpu.VMEM((2, HEAD_DIM, 1024), BF16)
    parts, logs = (3, 16, HEAD_DIM, 128), (3, 16, 1, 128)
    dma = pltpu.SemaphoreType.DMA
    hbm = pl.BlockSpec(memory_space=pl.ANY)
    smem = pl.BlockSpec(memory_space=pltpu.SMEM)
    return pl.pallas_call(
        kernel,
        out_shape=jax.ShapeDtypeStruct(queries.shape, BF16),
        in_specs=[smem, smem, hbm, hbm, hbm, hbm],
        out_specs=pl.BlockSpec(memory_space=pltpu.VMEM),
        scratch_shapes=[
            block, block, block, turned, block, block, block, block, block, turned,
            pltpu.VMEM(parts, BF16), pltpu.VMEM(logs, F32), pltpu.VMEM(parts, BF16), pltpu.VMEM(logs, F32),
            pltpu.VMEM((4, 8, HEAD_DIM, 256), F32), pltpu.VMEM((4, 8, 1, 256), F32), pltpu.VMEM((4, 8, 1, 256), F32),
            pltpu.VMEM((2, 1024, 256), F32), block,
            pltpu.VMEM(past.shape, BF16), pltpu.VMEM(queries.shape, F32), pltpu.VMEM((8, 2, 128, HEAD_DIM), BF16),
            dma((3,)), dma((3, 2, 8)), dma((3, 2)), dma((3, 16)), dma((2, 2)), dma((2, 16)),
            dma((3, 2)), dma((3, 2)), dma((3, 16)), dma((3, 16)), dma(()), dma((8, 2)), dma(()),
        ],
        compiler_params=pltpu.CompilerParams(collective_id=0, has_side_effects=True),
        name="attention",
    )(slot, table, queries, keys, values, past)


def shards(queries, keys, values, past_outputs, dwa_slot, dwa_table):
    return attention(dwa_slot, dwa_table, queries, keys, values, past_outputs)


def solution(mesh):
    tokens = P(("rep", "seq", "uly"), None)
    return jax.shard_map(
        shards,
        mesh=mesh,
        in_specs=(tokens, tokens, tokens, P(None, ("rep", "seq", "uly"), None), P(), P()),
        out_specs=tokens,
        check_vma=False,
    )
```

time: 141 us -> 68.3 us (0.48)
  the two profiles are of different devices: /device:TPU:352 before, /device:TPU:784 now
where the time goes in v2:
time: 68.3 us; the launch traced here: 68.1 us
  Pallas kernels  66.2 us (97%)
  local copies, waits for them, and re-layouts  1.88 us (3%)
    pallas_call x1, Pallas kernels, attention(): pl.pallas_call(kernel, out_shape=jax.ShapeDtypeStruct(queries.shape, BF16...  66.2 us
    unnamed x1, local copies, waits for them, and re-layouts  1.88 us

profile of v2, /device:TPU:784, one launch (start us, length us, event | category | flops | bytes accessed | tf_op | source)
XLA Modules:
  0.0 68.1 jit_solution(16380001369714640077)
XLA Ops:
  0.0 66.2 %attention.1 = bf16[128,2048]{1,0:T(8,128)(2,1)} custom-call(s32[2]{0:T(128)} %slot.1, f32[2,64]{1,0:T(2,128)} %table.1, bf16[128,2048]{1,0:T(8,128)(2,1)} %q_hbm.1, bf16[128,2048]{1,0:T(8,128)(2,1)} %k_hbm.1, bf16[128,2048]{1,0:T(8,128)(2,1)} %v_hbm.1, bf16[2,128,2048]{2,1,0:T(8,128)(2,1)} %past_hbm.1), custom_call_target="tpu_custom_call" | custom-call | tf_op jit(solution)/shard_map/attention/pallas_call | solution.py:370
  66.2 1.9 %copy.8 = bf16[128,2048]{1,0:T(8,128)(2,1)} copy(bf16[128,2048]{1,0:T(8,128)(2,1)} %attention.1) | data formatting | bytes 1048576

commit v3 on v2

--- a/solution.py
+++ b/solution.py
@@ -19,23 +19,36 @@
 MIRROR = tuple(PLACES.index((dy, (4 - dx) % 4)) for dy, dx in PLACES)
 
 MODES = ((1, 2), (0, 3))
-EXCHANGE = ((0, 0, 0, 4), (1, 0, 0, 8), (2, 0, 0, 8), (0, 0, 4, 8), (1, 1, 0, 8), (2, 1, 0, 8), (0, 1, 0, 8))
-
-STEPS = ("S0", "R1", "R2", "C3", "C2", "C1", "C0", "M2", "M1", "M0", "KV", "KF", "SK", "SV")
+EXCHANGE = (
+    32, 10, 11, 13, 8, 12, 15, 28, 22, 14, 38, 33, 18, 34, 37, 17, 36, 39, 23, 21, 45, 35, 29, 43,
+    27, 30, 26, 20, 46, 19, 44, 31, 47, 42, 41, 0, 24, 25, 6, 2, 16, 9, 1, 40, 7, 3, 4, 5,
+)
+
+STEPS = ("S0", "R1", "R2", "C3", "C2", "C1", "C0", "M2", "M1", "M0", "KV", "KF", "SK")
 ORDER = (
-    208, 192, 8, 1, 2, 193, 0, 3, 194, 196, 24, 195, 17, 198, 211, 16, 19, 199, 210, 18, 209, 212, 197, 4,
-    160, 5, 6, 215, 64, 7, 214, 96, 213, 40, 20, 65, 21, 99, 22, 81, 80, 23, 176, 49, 9, 114, 115, 10,
-    48, 11, 50, 113, 112, 12, 66, 13, 117, 161, 25, 116, 67, 131, 26, 130, 51, 27, 14, 15, 82, 118, 129, 119,
-    133, 41, 42, 132, 68, 43, 28, 83, 84, 101, 29, 30, 134, 135, 52, 69, 31, 53, 44, 45, 97, 120, 46, 98,
-    47, 121, 85, 122, 151, 150, 123, 54, 55, 138, 100, 148, 87, 70, 86, 124, 71, 125, 146, 126, 127, 139, 141, 145,
-    142, 143, 154, 140, 137, 102, 149, 103, 158, 157, 128, 155, 159, 147, 156, 153, 136, 144, 152,
+    8, 0, 10, 11, 13, 192, 12, 15, 14, 26, 198, 27, 194, 193, 29, 28, 31, 197, 30, 42, 199, 43, 45, 44,
+    195, 47, 46, 24, 196, 161, 53, 9, 2, 54, 69, 70, 3, 55, 7, 85, 5, 4, 71, 122, 25, 123, 18, 124,
+    86, 19, 160, 176, 125, 6, 96, 23, 98, 127, 87, 126, 20, 21, 139, 102, 140, 1, 138, 141, 68, 49, 40, 143,
+    41, 22, 142, 103, 65, 82, 16, 115, 114, 101, 50, 66, 116, 156, 17, 117, 52, 67, 81, 131, 51, 155, 132, 118,
+    100, 157, 48, 119, 99, 130, 121, 133, 64, 113, 120, 84, 83, 135, 80, 134, 159, 148, 149, 97, 137, 129, 158, 112,
+    151, 146, 136, 154, 147, 153, 150, 145, 128, 152, 144,
 )
 
 
+M0S = tuple(code % 16 for code in ORDER if STEPS[code // 16] == "M0")
+BATCHES = ((0, 8), (8, 10), (10, 12), (12, 13), (13, 14), (14, 15), (15, 16))
+
+
+def batch_of(chunk):
+    at = M0S.index(chunk)
+    return next(i for i, (first, last) in enumerate(BATCHES) if first <= at < last)
+
+
 def kernel(
-    slot, table, q_hbm, k_hbm, v_hbm, past_hbm, out,
-    qb, kb, vb, vt, q1, q2, q3, kf, vf, vft, o_in, l_in, o_out, l_out, acc, top, tot, scores, ready, past, base, came,
-    ex_send, ex_recv, q_send, q_recv, kv_send, kv_recv, o_send, l_send, o_recv, l_recv, f_send, f_recv, past_sem,
+    slot_hbm, table_hbm, q_hbm, k_hbm, v_hbm, past_hbm, out,
+    slot, table, qs, ks, vs, past, base, tally,
+    qb, kb, vb, vt, q1, q2, q3, kf, vf, vft, o_in, l_in, o_out, l_out, acc, top, tot, scores, ready, came,
+    stage_sem, ex_send, q_ex, kv_ex, q_send, q_recv, kv_send, kv_recv, o_send, o_recv, f_send, f_recv,
 ):
     z = lax.axis_index("seq")
     n_z = lax.axis_size("seq")
@@ -70,25 +83,39 @@
     def _():
         pl.semaphore_signal(barrier, inc=1, device_id=to_upper, device_id_type=MESH)
 
-    gathered = ((q_hbm, qb), (k_hbm, kb), (v_hbm, vb))
+    gathered = ((q_hbm, qs, qb), (k_hbm, ks, kb), (v_hbm, vs, vb))
+
+    def exchange_sem(t, h, p):
+        if t == 0:
+            return q_ex.at[h, p]
+        return kv_ex.at[h, p if MODES[h][0] else 0]
 
     def own_copy(t, h):
-        src, dst = gathered[t]
-        return pltpu.make_async_copy(src.at[:, columns_of(me, h)], dst.at[h, place_rows(0)], ex_recv.at[t, h, 0])
+        src, _staged, dst = gathered[t]
+        return pltpu.make_async_copy(src.at[:, columns_of(me, h)], dst.at[h, place_rows(0)], exchange_sem(t, h, 0))
 
     def exchange(t, h, p):
-        src, dst = gathered[t]
+        _src, staged, dst = gathered[t]
         to = peer(MIRROR[p])
         return pltpu.make_async_remote_copy(
-            src_ref=src.at[:, columns_of(to, h)], dst_ref=dst.at[h, place_rows(p)],
-            send_sem=ex_send.at[t], recv_sem=ex_recv.at[t, h, p], device_id={"uly": to}, device_id_type=MESH,
+            src_ref=staged.at[:, columns_of(to, h)], dst_ref=dst.at[h, place_rows(p)],
+            send_sem=ex_send, recv_sem=exchange_sem(t, h, p), device_id={"uly": to}, device_id_type=MESH,
         )
 
+    def stage(t):
+        return pltpu.make_async_copy(gathered[t][0], gathered[t][1], stage_sem.at[t])
+
+    stored = [
+        pltpu.make_async_copy(src, dst, stage_sem.at[3 + i])
+        for i, (src, dst) in enumerate(((past_hbm, past), (slot_hbm, slot), (table_hbm, table)))
+    ]
+    for t in range(3):
+        stage(t).start()
     for h in range(2):
         for t in range(3):
             own_copy(t, h).start()
-    past_copy = pltpu.make_async_copy(past_hbm, past, past_sem)
-    past_copy.start()
+    for copy in stored:
+        copy.start()
 
     @pl.when(z == 0)
     def _():
@@ -97,32 +124,40 @@
         kf[...] = jnp.zeros_like(kf)
         vf[...] = jnp.zeros_like(vf)
 
-    past_copy.wait()
-    coefs = [table[0, slot[i]] + table[1, slot[i]] for i in range(2)]
-
-    def stored_sum(i, carry):
-        rows = pl.ds(pl.multiple_of(i * 16, 16), 16)
-        base[rows] = past[0, rows].astype(F32) * coefs[0] + past[1, rows].astype(F32) * coefs[1]
-        return carry
-
-    lax.fori_loop(0, 8, stored_sum, 0)
-
+    def stored_sum():
+        for copy in stored:
+            copy.wait()
+        coefs = [table[0, slot[i]] + table[1, slot[i]] for i in range(2)]
+
+        def rows_sum(i, carry):
+            rows = pl.ds(pl.multiple_of(i * 16, 16), 16)
+            base[rows] = past[0, rows].astype(F32) * coefs[0] + past[1, rows].astype(F32) * coefs[1]
+            return carry
+
+        lax.fori_loop(0, 8, rows_sum, 0)
+
+    for t in range(3):
+        stage(t).wait()
     pl.semaphore_wait(barrier, 7 + jnp.where(below, 1, 0) + jnp.where(above, 1, 0))
 
-    for t, h, first, last in EXCHANGE:
-        for p in range(max(first, 1), last):
-            exchange(t, h, p).start()
+    for code in EXCHANGE:
+        if code % 8:
+            exchange(code // 16, code // 8 % 2, code % 8).start()
 
     blocks = (qb, q1, q2, q3)
 
     def split(chunk):
         return chunk // 8, place_rows(chunk % 8)
+
+    def chunk_base(level):
+        return 8 if level == 2 and MODES[0][1] < 3 else 0
 
     def down(level, chunk):
         h, rows = split(chunk)
         return pltpu.make_async_remote_copy(
             src_ref=blocks[level].at[h, rows], dst_ref=blocks[level + 1].at[h, rows],
-            send_sem=q_send.at[level, h], recv_sem=q_recv.at[level, chunk], device_id=to_lower, device_id_type=MESH,
+            send_sem=q_send.at[level], recv_sem=q_recv.at[level * 16 + chunk - chunk_base(level)],
+            device_id=to_lower, device_id_type=MESH,
         )
 
     def forward(t, chunk):
@@ -130,25 +165,28 @@
         src, dst = ((kb, kf), (vb, vf))[t]
         return pltpu.make_async_remote_copy(
             src_ref=src.at[h, rows], dst_ref=dst.at[h, rows],
-            send_sem=kv_send.at[t, h], recv_sem=kv_recv.at[t, chunk], device_id=to_upper, device_id_type=MESH,
+            send_sem=kv_send.at[h], recv_sem=kv_recv.at[h], device_id=to_upper, device_id_type=MESH,
         )
 
     def up(level, chunk):
-        h = chunk // 8
+        at = level * 16 + chunk - chunk_base(level)
         return [
             pltpu.make_async_remote_copy(
                 src_ref=src.at[level, chunk], dst_ref=dst.at[level, chunk],
-                send_sem=send.at[level, h], recv_sem=recv.at[level, chunk], device_id=to_upper, device_id_type=MESH,
+                send_sem=o_send.at[level], recv_sem=o_recv.at[at], device_id=to_upper, device_id_type=MESH,
             )
-            for src, dst, send, recv in ((o_out, o_in, o_send, o_recv), (l_out, l_in, l_send, l_recv))
+            for src, dst in ((o_out, o_in), (l_out, l_in))
         ]
+
+    def arrived(semaphore, count):
+        pltpu.make_async_copy(tally.at[pl.ds(0, count)], tally.at[pl.ds(0, count)], semaphore).wait()
 
     def finish(chunk):
         h, rows = split(chunk)
         place = chunk % 8
         return pltpu.make_async_remote_copy(
             src_ref=ready.at[h, rows], dst_ref=came.at[MIRROR[place], h], send_sem=f_send,
-            recv_sem=f_recv.at[MIRROR[place], h], device_id={"uly": peer(place)}, device_id_type=MESH,
+            recv_sem=f_recv.at[batch_of(chunk)], device_id={"uly": peer(place)}, device_id_type=MESH,
         )
 
     done = set()
@@ -173,17 +211,21 @@
     exists = [None, has(1), has(2), has(3)]
     came_up = [below, has(1) & below, has(2) & below]
 
-    def gathered_rows(t, h, p):
-        copy = own_copy(t, h).wait if p == 0 else exchange(t, h, p).wait_recv
-        return (None, ("gathered", t, h, p), [copy])
-
     def queries(level, chunk):
+        h, p = chunk // 8, chunk % 8
         if level == 0:
-            return gathered_rows(0, chunk // 8, chunk % 8)
-        return (exists[level], ("down", level, chunk), [down(level - 1, chunk).wait_recv])
+            return (None, ("queries", h, p), [functools.partial(arrived, exchange_sem(0, h, p), 64)])
+        at = (level - 1) * 16 + chunk - chunk_base(level - 1)
+        return (exists[level], ("down", level, chunk), [functools.partial(arrived, q_recv.at[at], 64)])
+
+    def keys_values(h, p):
+        if MODES[h][0]:
+            return (None, ("keys", h, p), [functools.partial(arrived, exchange_sem(1, h, p), 128)])
+        return (None, ("keys", h), [functools.partial(arrived, exchange_sem(1, h, p), 1024)])
 
     def part(level, chunk):
-        return (came_up[level], ("up", level, chunk), [copy.wait_recv for copy in up(level, chunk)])
+        at = level * 16 + chunk - chunk_base(level)
+        return (came_up[level], ("up", level, chunk), [functools.partial(arrived, o_recv.at[at], 65)])
 
     def first_stage(step, pair, buffer):
         level = int(step[1])
@@ -279,22 +321,23 @@
         weighted = acc[level, pair, :, lanes] * a + new_weighted * b
         return weighted / total, most + jnp.log2(total)
 
-    for code in ORDER:
-        step, which = STEPS[code // 16], code % 16
+    def run(step, which):
         if step in ("S0", "R1", "R2"):
             level = STEPS.index(step)
             expect(queries(level, which))
             pl.when(has(level) & below)(down(level, which).start)
-        elif step in ("SK", "SV"):
-            t = STEPS.index(step) - STEPS.index("SK")
-            expect(gathered_rows(t + 1, which // 8, which % 8))
-            pl.when(above)(forward(t, which).start)
+        elif step == "SK":
+            expect(keys_values(which // 8, which % 8))
+
+            @pl.when(above)
+            def _():
+                for t in range(2):
+                    forward(t, which).start()
         elif step == "KV":
-            expect(*(gathered_rows(t, which, p) for t in (1, 2) for p in range(8)))
+            expect(*(keys_values(which, p) for p in range(8)))
             vt[which] = jnp.transpose(vb[which])
         elif step == "KF":
-            chunks = range(which * 8, which * 8 + 8)
-            expect(*((below, ("kf", t, c), [forward(t, c).wait_recv]) for t in (0, 1) for c in chunks))
+            expect((below, ("kf", which), [functools.partial(arrived, kv_recv.at[which], 1024)]))
             vft[which] = jnp.transpose(vf[which])
         elif step[0] == "C":
             level = int(step[1])
@@ -328,58 +371,58 @@
                 for copy in up(level - 1, which):
                     copy.start()
 
+    summed = False
     for code in ORDER:
         step, which = STEPS[code // 16], code % 16
-        if step == "M0":
-            h, place = which // 8, MIRROR[which % 8]
-            if place:
-                pltpu.make_async_remote_copy(
-                    src_ref=ready.at[h, place_rows(place)], dst_ref=came.at[place, h], send_sem=f_send,
-                    recv_sem=f_recv.at[place, h], device_id={"uly": peer(place)}, device_id_type=MESH,
-                ).wait_recv()
+        if not summed and (step not in ("S0", "SK") or which % 8):
+            stored_sum()
+            summed = True
+        run(step, which)
+
+    for batch, (first, last) in enumerate(BATCHES):
+        chunks = M0S[first:last]
+        remote = sum(1 for chunk in chunks if chunk % 8)
+        if remote:
+            arrived(f_recv.at[batch], remote * 64)
+        for chunk in chunks:
+            h, place = chunk // 8, MIRROR[chunk % 8]
             lanes = columns_of(peer(place), h)
             out[:, lanes] = (base[:, lanes] + came[place, h].astype(F32)).astype(BF16)
 
-    for t, (_src, dst) in enumerate(gathered):
-        sent = dst.at[:, pl.ds(0, 896)]
-        pltpu.make_async_copy(sent, sent, ex_send.at[t]).wait()
+    sent = scores.at[:, pl.ds(0, 672)]
+    pltpu.make_async_copy(sent, sent, ex_send).wait()
     sent = ready.at[:, pl.ds(0, 896)]
     pltpu.make_async_copy(sent, sent, f_send).wait()
-
-    def all_left(condition, sent, sem):
-        pl.when(condition)(pltpu.make_async_copy(sent, sent, sem).wait)
-
-    for h, (up_hops, down_hops) in enumerate(MODES):
-        chunks = pl.ds(h * 8, 8)
-        for level in range(down_hops):
-            all_left(has(level) & below, blocks[level].at[h], q_send.at[level, h])
-            all_left(has(level + 1), o_out.at[level, chunks], o_send.at[level, h])
-            all_left(has(level + 1), l_out.at[level, chunks], l_send.at[level, h])
+    for level in range(3):
+        heads = sum(1 for _up_hops, down_hops in MODES if down_hops > level)
+        if heads:
+            pl.when(has(level) & below)(functools.partial(arrived, q_send.at[level], 512 * heads))
+            pl.when(has(level + 1))(functools.partial(arrived, o_send.at[level], 520 * heads))
+    for h, (up_hops, _down_hops) in enumerate(MODES):
         if up_hops:
-            all_left(above, kb.at[h], kv_send.at[0, h])
-            all_left(above, vb.at[h], kv_send.at[1, h])
+            pl.when(above)(functools.partial(arrived, kv_send.at[h], 1024))
 
 
 def attention(slot, table, queries, keys, values, past):
     block = pltpu.VMEM((2, 1024, HEAD_DIM), BF16)
     turned = pltpu.VMEM((2, HEAD_DIM, 1024), BF16)
+    staged = pltpu.VMEM(queries.shape, BF16)
     parts, logs = (3, 16, HEAD_DIM, 128), (3, 16, 1, 128)
     dma = pltpu.SemaphoreType.DMA
-    hbm = pl.BlockSpec(memory_space=pl.ANY)
-    smem = pl.BlockSpec(memory_space=pltpu.SMEM)
+    chunks = 32 + 8 * sum(1 for _up_hops, down_hops in MODES if down_hops == 3)
     return pl.pallas_call(
         kernel,
-        out_shape=jax.ShapeDtypeStruct(queries.shape, BF16),
-        in_specs=[smem, smem, hbm, hbm, hbm, hbm],
-        out_specs=pl.BlockSpec(memory_space=pltpu.VMEM),
+        out_shape=pltpu.VMEM(queries.shape, BF16),
+        in_specs=[pl.BlockSpec(memory_space=pl.ANY)] * 6,
         scratch_shapes=[
+            pltpu.SMEM(slot.shape, jnp.int32), pltpu.SMEM(table.shape, F32), staged, staged, staged,
+            pltpu.VMEM(past.shape, BF16), pltpu.VMEM(queries.shape, F32), pltpu.VMEM((1040, 1, 128), F32),
             block, block, block, turned, block, block, block, block, block, turned,
             pltpu.VMEM(parts, BF16), pltpu.VMEM(logs, F32), pltpu.VMEM(parts, BF16), pltpu.VMEM(logs, F32),
             pltpu.VMEM((4, 8, HEAD_DIM, 256), F32), pltpu.VMEM((4, 8, 1, 256), F32), pltpu.VMEM((4, 8, 1, 256), F32),
-            pltpu.VMEM((2, 1024, 256), F32), block,
-            pltpu.VMEM(past.shape, BF16), pltpu.VMEM(queries.shape, F32), pltpu.VMEM((8, 2, 128, HEAD_DIM), BF16),
-            dma((3,)), dma((3, 2, 8)), dma((3, 2)), dma((3, 16)), dma((2, 2)), dma((2, 16)),
-            dma((3, 2)), dma((3, 2)), dma((3, 16)), dma((3, 16)), dma(()), dma((8, 2)), dma(()),
+            pltpu.VMEM((2, 1024, 256), F32), block, pltpu.VMEM((8, 2, 128, HEAD_DIM), BF16),
+            dma((6,)), dma(()), dma((2, 8)), dma((2, 8)), dma((3,)), dma((chunks,)), dma((2,)), dma((2,)),
+            dma((3,)), dma((chunks,)), dma(()), dma((len(BATCHES),)),
         ],
         compiler_params=pltpu.CompilerParams(collective_id=0, has_side_effects=True),
         name="attention",

time: 68.3 us -> 61.4 us (0.90)
  the two profiles are of different devices: /device:TPU:784 before, /device:TPU:64 now
where the time goes in v3:
time: 61.4 us; the launch traced here: 61.3 us
  Pallas kernels  60.5 us (99%)
  local copies, waits for them, and re-layouts  0.8 us (1%)
    pallas_call x1, Pallas kernels, attention(): pl.pallas_call(kernel, out_shape=pltpu.VMEM(queries.shape, BF16), in_spec...  60.5 us

profile of v3, /device:TPU:64, one launch (start us, length us, event | category | flops | bytes accessed | tf_op | source)
XLA Modules:
  0.0 61.3 jit_solution(5568950211032135150)
XLA Ops:
  0.0 60.5 %attention.1 = bf16[128,2048]{1,0:T(8,128)(2,1)S(1)} custom-call(s32[2]{0:T(128)} %slot_hbm.1, f32[2,64]{1,0:T(2,128)} %table_hbm.1, bf16[128,2048]{1,0:T(8,128)(2,1)} %q_hbm.1, bf16[128,2048]{1,0:T(8,128)(2,1)} %k_hbm.1, bf16[128,2048]{1,0:T(8,128)(2,1)} %v_hbm.1, bf16[2,128,2048]{2,1,0:T(8,128)(2,1)} %past_hbm.1), custom_call_target="tpu_custom_call" | custom-call | tf_op jit(solution)/shard_map/attention/pallas_call | solution.py:413
  60.5 0.8 %copy.8 = bf16[128,2048]{1,0:T(8,128)(2,1)} copy(bf16[128,2048]{1,0:T(8,128)(2,1)S(1)} %attention.1) | data formatting | bytes 1048576

commit v4 on v3

--- a/solution.py
+++ b/solution.py
@@ -19,24 +19,25 @@
 MIRROR = tuple(PLACES.index((dy, (4 - dx) % 4)) for dy, dx in PLACES)
 
 MODES = ((1, 2), (0, 3))
+RAISED = next(h for h, (up_hops, _down_hops) in enumerate(MODES) if up_hops)
 EXCHANGE = (
-    32, 10, 11, 13, 8, 12, 15, 28, 22, 14, 38, 33, 18, 34, 37, 17, 36, 39, 23, 21, 45, 35, 29, 43,
-    27, 30, 26, 20, 46, 19, 44, 31, 47, 42, 41, 0, 24, 25, 6, 2, 16, 9, 1, 40, 7, 3, 4, 5,
+    9, 11, 10, 14, 15, 25, 7, 2, 6, 19, 1, 34, 39, 22, 4, 47, 29, 27, 43, 44, 31, 26, 13, 5,
+    12, 20, 18, 35, 28, 42, 3, 45, 30, 46, 41, 37, 38, 21, 36, 33, 23, 17,
 )
 
-STEPS = ("S0", "R1", "R2", "C3", "C2", "C1", "C0", "M2", "M1", "M0", "KV", "KF", "SK")
+STEPS = ("S0", "R1", "R2", "C3", "C2", "C1", "C0", "M2", "M1", "M0", "KV", "KF", "SK", "XK", "XI")
 ORDER = (
-    8, 0, 10, 11, 13, 192, 12, 15, 14, 26, 198, 27, 194, 193, 29, 28, 31, 197, 30, 42, 199, 43, 45, 44,
-    195, 47, 46, 24, 196, 161, 53, 9, 2, 54, 69, 70, 3, 55, 7, 85, 5, 4, 71, 122, 25, 123, 18, 124,
-    86, 19, 160, 176, 125, 6, 96, 23, 98, 127, 87, 126, 20, 21, 139, 102, 140, 1, 138, 141, 68, 49, 40, 143,
-    41, 22, 142, 103, 65, 82, 16, 115, 114, 101, 50, 66, 116, 156, 17, 117, 52, 67, 81, 131, 51, 155, 132, 118,
-    100, 157, 48, 119, 99, 130, 121, 133, 64, 113, 120, 84, 83, 135, 80, 134, 159, 148, 149, 97, 137, 129, 158, 112,
-    151, 146, 136, 154, 147, 153, 150, 145, 128, 152, 144,
+    224, 0, 8, 193, 9, 11, 196, 197, 226, 194, 10, 192, 14, 228, 15, 227, 195, 199, 24, 25, 27, 26, 225, 30,
+    31, 40, 41, 43, 42, 198, 46, 47, 161, 87, 13, 215, 210, 213, 229, 12, 5, 4, 84, 7, 52, 6, 53, 55,
+    29, 1, 68, 69, 28, 71, 211, 212, 121, 214, 122, 120, 126, 20, 209, 21, 103, 23, 102, 127, 100, 22, 123, 101,
+    137, 45, 160, 85, 44, 138, 98, 142, 70, 143, 3, 176, 16, 50, 139, 2, 66, 82, 17, 117, 67, 116, 51, 118,
+    158, 54, 19, 119, 86, 153, 96, 18, 133, 99, 83, 132, 64, 48, 81, 134, 80, 125, 113, 124, 65, 49, 135, 115,
+    150, 114, 129, 140, 97, 141, 154, 151, 131, 159, 155, 130, 148, 112, 145, 149, 157, 136, 156, 147, 146, 128, 152, 144,
 )
 
 
 M0S = tuple(code % 16 for code in ORDER if STEPS[code // 16] == "M0")
-BATCHES = ((0, 8), (8, 10), (10, 12), (12, 13), (13, 14), (14, 15), (15, 16))
+BATCHES = ((0, 8), (8, 11), (11, 13), (13, 14), (14, 15), (15, 16))
 
 
 def batch_of(chunk):
@@ -47,14 +48,15 @@
 def kernel(
     slot_hbm, table_hbm, q_hbm, k_hbm, v_hbm, past_hbm, out,
     slot, table, qs, ks, vs, past, base, tally,
-    qb, kb, vb, vt, q1, q2, q3, kf, vf, vft, o_in, l_in, o_out, l_out, acc, top, tot, scores, ready, came,
-    stage_sem, ex_send, q_ex, kv_ex, q_send, q_recv, kv_send, kv_recv, o_send, o_recv, f_send, f_recv,
+    qb, kb, vb, vt, q1, q2, q3, raised, kf, vf, vft, o_in, l_in, o_out, l_out, acc, top, tot, scores, ready, came,
+    stage_sem, ex_send, q_ex, kv_ex, q_send, q_recv, kv_send, raised_recv, kf_recv, o_send, f_send, f_recv,
 ):
     z = lax.axis_index("seq")
     n_z = lax.axis_size("seq")
     me = lax.axis_index("uly")
     y, x = me // 4, lax.rem(me, 4)
     below, above = z > 0, z < n_z - 1
+    far_below = z > 1
     to_lower = {"seq": jnp.maximum(z - 1, 0)}
     to_upper = {"seq": jnp.minimum(z + 1, n_z - 1)}
 
@@ -79,7 +81,7 @@
     def _():
         pl.semaphore_signal(barrier, inc=1, device_id=to_lower, device_id_type=MESH)
 
-    @pl.when(above)
+    @pl.when(above & below)
     def _():
         pl.semaphore_signal(barrier, inc=1, device_id=to_upper, device_id_type=MESH)
 
@@ -88,7 +90,7 @@
     def exchange_sem(t, h, p):
         if t == 0:
             return q_ex.at[h, p]
-        return kv_ex.at[h, p if MODES[h][0] else 0]
+        return kv_ex.at[h]
 
     def own_copy(t, h):
         src, _staged, dst = gathered[t]
@@ -99,7 +101,7 @@
         to = peer(MIRROR[p])
         return pltpu.make_async_remote_copy(
             src_ref=staged.at[:, columns_of(to, h)], dst_ref=dst.at[h, place_rows(p)],
-            send_sem=ex_send, recv_sem=exchange_sem(t, h, p), device_id={"uly": to}, device_id_type=MESH,
+            send_sem=ex_send.at[0], recv_sem=exchange_sem(t, h, p), device_id={"uly": to}, device_id_type=MESH,
         )
 
     def stage(t):
@@ -117,8 +119,7 @@
     for copy in stored:
         copy.start()
 
-    @pl.when(z == 0)
-    def _():
+    def no_parts():
         o_in[...] = jnp.zeros_like(o_in)
         l_in[...] = jnp.full_like(l_in, -1e30)
         kf[...] = jnp.zeros_like(kf)
@@ -136,13 +137,7 @@
 
         lax.fori_loop(0, 8, rows_sum, 0)
 
-    for t in range(3):
-        stage(t).wait()
-    pl.semaphore_wait(barrier, 7 + jnp.where(below, 1, 0) + jnp.where(above, 1, 0))
-
-    for code in EXCHANGE:
-        if code % 8:
-            exchange(code // 16, code // 8 % 2, code % 8).start()
+    pl.semaphore_wait(barrier, 7 + jnp.where(far_below, 1, 0) + jnp.where(above, 1, 0))
 
     blocks = (qb, q1, q2, q3)
 
@@ -151,29 +146,39 @@
 
     def chunk_base(level):
         return 8 if level == 2 and MODES[0][1] < 3 else 0
+
+    def query_sem(level, chunk):
+        if level == 0:
+            return q_ex.at[chunk // 8, chunk % 8]
+        return q_recv.at[(level - 1) * 16 + chunk - chunk_base(level - 1)]
 
     def down(level, chunk):
         h, rows = split(chunk)
         return pltpu.make_async_remote_copy(
             src_ref=blocks[level].at[h, rows], dst_ref=blocks[level + 1].at[h, rows],
-            send_sem=q_send.at[level], recv_sem=q_recv.at[level * 16 + chunk - chunk_base(level)],
-            device_id=to_lower, device_id_type=MESH,
+            send_sem=q_send.at[level], recv_sem=query_sem(level + 1, chunk), device_id=to_lower, device_id_type=MESH,
         )
 
-    def forward(t, chunk):
-        h, rows = split(chunk)
-        src, dst = ((kb, kf), (vb, vf))[t]
+    def raise_piece(t, p):
+        _src, staged, _dst = gathered[t]
+        dst = (None, kf, vf)[t].at[place_rows(0)] if p == 0 else raised.at[t - 1, p]
         return pltpu.make_async_remote_copy(
-            src_ref=src.at[h, rows], dst_ref=dst.at[h, rows],
-            send_sem=kv_send.at[h], recv_sem=kv_recv.at[h], device_id=to_upper, device_id_type=MESH,
+            src_ref=staged.at[:, columns_of(peer(p), RAISED)], dst_ref=dst, send_sem=kv_send,
+            recv_sem=kf_recv if p == 0 else raised_recv.at[p], device_id=to_upper, device_id_type=MESH,
         )
 
+    def pass_on(t, p):
+        dst = (None, kf, vf)[t]
+        return pltpu.make_async_remote_copy(
+            src_ref=raised.at[t - 1, p], dst_ref=dst.at[place_rows(MIRROR[p])], send_sem=ex_send.at[1],
+            recv_sem=kf_recv, device_id={"uly": peer(p)}, device_id_type=MESH,
+        )
+
     def up(level, chunk):
-        at = level * 16 + chunk - chunk_base(level)
         return [
             pltpu.make_async_remote_copy(
                 src_ref=src.at[level, chunk], dst_ref=dst.at[level, chunk],
-                send_sem=o_send.at[level], recv_sem=o_recv.at[at], device_id=to_upper, device_id_type=MESH,
+                send_sem=o_send.at[level], recv_sem=query_sem(level, chunk), device_id=to_upper, device_id_type=MESH,
             )
             for src, dst in ((o_out, o_in), (l_out, l_in))
         ]
@@ -212,32 +217,26 @@
     came_up = [below, has(1) & below, has(2) & below]
 
     def queries(level, chunk):
-        h, p = chunk // 8, chunk % 8
-        if level == 0:
-            return (None, ("queries", h, p), [functools.partial(arrived, exchange_sem(0, h, p), 64)])
-        at = (level - 1) * 16 + chunk - chunk_base(level - 1)
-        return (exists[level], ("down", level, chunk), [functools.partial(arrived, q_recv.at[at], 64)])
-
-    def keys_values(h, p):
-        if MODES[h][0]:
-            return (None, ("keys", h, p), [functools.partial(arrived, exchange_sem(1, h, p), 128)])
-        return (None, ("keys", h), [functools.partial(arrived, exchange_sem(1, h, p), 1024)])
+        return (exists[level], ("down", level, chunk), [functools.partial(arrived, query_sem(level, chunk), 64)])
 
     def part(level, chunk):
-        at = level * 16 + chunk - chunk_base(level)
-        return (came_up[level], ("up", level, chunk), [functools.partial(arrived, o_recv.at[at], 65)])
+        return (came_up[level], ("up", level, chunk), [functools.partial(arrived, query_sem(level, chunk), 65)])
+
+    def in_vmem(t):
+        return (None, ("in_vmem", t), [lambda: stage(t).wait()])
 
     def first_stage(step, pair, buffer):
         level = int(step[1])
         h, rows = pair // 4, pl.ds((pair % 4) * 256, 256)
-        keys = kb
         source = blocks[level]
-        if level == 3 and MODES[h][0] == 1:
-            keys, source = kf, q2
+        if level == 3 and h == RAISED:
+            source = q2
         query = source[h, rows]
         tops = []
         for b in range(4):
-            s = lax.dot_general(keys[h, pl.ds(b * 256, 256)], query, NT, preferred_element_type=F32)
+            of_keys = pl.ds(b * 256, 256)
+            keys = kf[of_keys] if level == 3 and h == RAISED else kb[h, of_keys]
+            s = lax.dot_general(keys, query, NT, preferred_element_type=F32)
             if level == 0:
                 key_row = lax.broadcasted_iota(jnp.int32, (256, 1), 0)
                 query_row = lax.broadcasted_iota(jnp.int32, (1, 256), 1)
@@ -253,15 +252,14 @@
     def second_stage(step, pair, buffer, highest):
         level = int(step[1])
         h = pair // 4
-        values = vft if level == 3 and MODES[h][0] == 1 else vt
         total = jnp.zeros((8, 256), F32)
         weighted = None
         for b in range(4):
             prob = jnp.exp2((scores[buffer, pl.ds(b * 256, 256)] - highest) * SCALE)
             total += jnp.sum(prob.reshape(32, 8, 256), axis=0)
-            term = lax.dot_general(
-                values[h, :, pl.ds(b * 256, 256)], prob.astype(BF16), NN, preferred_element_type=F32
-            )
+            of_keys = pl.ds(b * 256, 256)
+            values = vft[:, of_keys] if level == 3 and h == RAISED else vt[h, :, of_keys]
+            term = lax.dot_general(values, prob.astype(BF16), NN, preferred_element_type=F32)
             weighted = term if weighted is None else weighted + term
         return weighted, jnp.sum(total, axis=0, keepdims=True)
 
@@ -321,24 +319,47 @@
         weighted = acc[level, pair, :, lanes] * a + new_weighted * b
         return weighted / total, most + jnp.log2(total)
 
+    held = []
+
     def run(step, which):
+        nonlocal held
         if step in ("S0", "R1", "R2"):
             level = STEPS.index(step)
             expect(queries(level, which))
-            pl.when(has(level) & below)(down(level, which).start)
+            if held is None:
+                pl.when(has(level) & below)(down(level, which).start)
+            else:
+                pl.when(has(level) & far_below)(down(level, which).start)
+                held.append((level, which))
+        elif step == "XI":
+            for code in EXCHANGE[which * 7 : which * 7 + 7]:
+                expect(in_vmem(code // 16))
+                exchange(code // 16, code // 8 % 2, code % 8).start()
         elif step == "SK":
-            expect(keys_values(which // 8, which % 8))
+            expect(in_vmem(1), in_vmem(2))
 
             @pl.when(above)
             def _():
-                for t in range(2):
-                    forward(t, which).start()
+                for t in (1, 2):
+                    raise_piece(t, which).start()
+        elif step == "XK":
+            expect((below, ("raised", which), [functools.partial(arrived, raised_recv.at[which], 128)]))
+
+            @pl.when(below)
+            def _():
+                for t in (1, 2):
+                    pass_on(t, which).start()
+
+            if held is not None:
+                for level, chunk in held:
+                    pl.when(has(level) & (z == 1))(down(level, chunk).start)
+                held = None
         elif step == "KV":
-            expect(*(keys_values(which, p) for p in range(8)))
+            expect((None, ("keys", which), [functools.partial(arrived, kv_ex.at[which], 1024)]))
             vt[which] = jnp.transpose(vb[which])
         elif step == "KF":
-            expect((below, ("kf", which), [functools.partial(arrived, kv_recv.at[which], 1024)]))
-            vft[which] = jnp.transpose(vf[which])
+            expect((below, ("raised",), [functools.partial(arrived, kf_recv, 1024)]))
+            vft[...] = jnp.transpose(vf[...])
         elif step[0] == "C":
             level = int(step[1])
             if level == 3 and MODES[which // 4][0] == 1:
@@ -374,7 +395,8 @@
     summed = False
     for code in ORDER:
         step, which = STEPS[code // 16], code % 16
-        if not summed and (step not in ("S0", "SK") or which % 8):
+        if not summed and step not in ("XI", "SK") and which % 8:
+            pl.when(z == 0)(no_parts)
             stored_sum()
             summed = True
         run(step, which)
@@ -390,17 +412,15 @@
             out[:, lanes] = (base[:, lanes] + came[place, h].astype(F32)).astype(BF16)
 
     sent = scores.at[:, pl.ds(0, 672)]
-    pltpu.make_async_copy(sent, sent, ex_send).wait()
+    pltpu.make_async_copy(sent, sent, ex_send.at[0]).wait()
     sent = ready.at[:, pl.ds(0, 896)]
     pltpu.make_async_copy(sent, sent, f_send).wait()
+    pl.when(below)(functools.partial(arrived, ex_send.at[1], 896))
+    pl.when(above)(functools.partial(arrived, kv_send, 1024))
     for level in range(3):
         heads = sum(1 for _up_hops, down_hops in MODES if down_hops > level)
-        if heads:
-            pl.when(has(level) & below)(functools.partial(arrived, q_send.at[level], 512 * heads))
-            pl.when(has(level + 1))(functools.partial(arrived, o_send.at[level], 520 * heads))
-    for h, (up_hops, _down_hops) in enumerate(MODES):
-        if up_hops:
-            pl.when(above)(functools.partial(arrived, kv_send.at[h], 1024))
+        pl.when(has(level) & below)(functools.partial(arrived, q_send.at[level], 512 * heads))
+        pl.when(has(level + 1))(functools.partial(arrived, o_send.at[level], 520 * heads))
 
 
 def attention(slot, table, queries, keys, values, past):
@@ -417,12 +437,13 @@
         scratch_shapes=[
             pltpu.SMEM(slot.shape, jnp.int32), pltpu.SMEM(table.shape, F32), staged, staged, staged,
             pltpu.VMEM(past.shape, BF16), pltpu.VMEM(queries.shape, F32), pltpu.VMEM((1040, 1, 128), F32),
-            block, block, block, turned, block, block, block, block, block, turned,
+            block, block, block, turned, block, block, block, pltpu.VMEM((2, 8, 128, HEAD_DIM), BF16),
+            pltpu.VMEM((1024, HEAD_DIM), BF16), pltpu.VMEM((1024, HEAD_DIM), BF16), pltpu.VMEM((HEAD_DIM, 1024), BF16),
             pltpu.VMEM(parts, BF16), pltpu.VMEM(logs, F32), pltpu.VMEM(parts, BF16), pltpu.VMEM(logs, F32),
             pltpu.VMEM((4, 8, HEAD_DIM, 256), F32), pltpu.VMEM((4, 8, 1, 256), F32), pltpu.VMEM((4, 8, 1, 256), F32),
             pltpu.VMEM((2, 1024, 256), F32), block, pltpu.VMEM((8, 2, 128, HEAD_DIM), BF16),
-            dma((6,)), dma(()), dma((2, 8)), dma((2, 8)), dma((3,)), dma((chunks,)), dma((2,)), dma((2,)),
-            dma((3,)), dma((chunks,)), dma(()), dma((len(BATCHES),)),
+            dma((6,)), dma((2,)), dma((2, 8)), dma((2,)), dma((3,)), dma((chunks,)), dma(()), dma((8,)), dma(()),
+            dma((3,)), dma(()), dma((len(BATCHES),)),
         ],
         compiler_params=pltpu.CompilerParams(collective_id=0, has_side_effects=True),
         name="attention",

time: 61.4 us -> 68.8 us (1.12)
  the two profiles are of different devices: /device:TPU:64 before, /device:TPU:96 now
where the time goes in v4:
time: 68.8 us; the launch traced here: 68.7 us
  Pallas kernels  67.9 us (99%)
  local copies, waits for them, and re-layouts  0.8 us (1%)
    pallas_call x1, Pallas kernels, attention(): pl.pallas_call(kernel, out_shape=pltpu.VMEM(queries.shape, BF16), in_spec...  67.9 us

profile of v4, /device:TPU:96, one launch (start us, length us, event | category | flops | bytes accessed | tf_op | source)
XLA Modules:
  0.0 68.7 jit_solution(15206176149791298428)
XLA Ops:
  0.0 67.9 %attention.1 = bf16[128,2048]{1,0:T(8,128)(2,1)S(1)} custom-call(s32[2]{0:T(128)} %slot_hbm.1, f32[2,64]{1,0:T(2,128)} %table_hbm.1, bf16[128,2048]{1,0:T(8,128)(2,1)} %q_hbm.1, bf16[128,2048]{1,0:T(8,128)(2,1)} %k_hbm.1, bf16[128,2048]{1,0:T(8,128)(2,1)} %v_hbm.1, bf16[2,128,2048]{2,1,0:T(8,128)(2,1)} %past_hbm.1), custom_call_target="tpu_custom_call" | custom-call | tf_op jit(solution)/shard_map/attention/pallas_call | solution.py:433
  67.9 0.8 %copy.8 = bf16[128,2048]{1,0:T(8,128)(2,1)} copy(bf16[128,2048]{1,0:T(8,128)(2,1)S(1)} %attention.1) | data formatting | bytes 1048576

commit v5 on v4

--- a/solution.py
+++ b/solution.py
@@ -56,7 +56,7 @@
     me = lax.axis_index("uly")
     y, x = me // 4, lax.rem(me, 4)
     below, above = z > 0, z < n_z - 1
-    far_below = z > 1
+    far_below = below
     to_lower = {"seq": jnp.maximum(z - 1, 0)}
     to_upper = {"seq": jnp.minimum(z + 1, n_z - 1)}
 
@@ -81,7 +81,7 @@
     def _():
         pl.semaphore_signal(barrier, inc=1, device_id=to_lower, device_id_type=MESH)
 
-    @pl.when(above & below)
+    @pl.when(above)
     def _():
         pl.semaphore_signal(barrier, inc=1, device_id=to_upper, device_id_type=MESH)
 
@@ -319,7 +319,7 @@
         weighted = acc[level, pair, :, lanes] * a + new_weighted * b
         return weighted / total, most + jnp.log2(total)
 
-    held = []
+    held = None
 
     def run(step, which):
         nonlocal held

time: 68.8 us -> 58.8 us (0.85)
  the two profiles are of different devices: /device:TPU:96 before, /device:TPU:64 now
where the time goes in v5:
time: 58.8 us; the launch traced here: 58.7 us
  Pallas kernels  57.9 us (98%)
  local copies, waits for them, and re-layouts  0.8 us (1%)
    pallas_call x1, Pallas kernels, attention(): pl.pallas_call(kernel, out_shape=pltpu.VMEM(queries.shape, BF16), in_spec...  57.9 us

profile of v5, /device:TPU:64, one launch (start us, length us, event | category | flops | bytes accessed | tf_op | source)
XLA Modules:
  0.0 58.7 jit_solution(3524664414626924237)
XLA Ops:
  0.0 57.9 %attention.1 = bf16[128,2048]{1,0:T(8,128)(2,1)S(1)} custom-call(s32[2]{0:T(128)} %slot_hbm.1, f32[2,64]{1,0:T(2,128)} %table_hbm.1, bf16[128,2048]{1,0:T(8,128)(2,1)} %q_hbm.1, bf16[128,2048]{1,0:T(8,128)(2,1)} %k_hbm.1, bf16[128,2048]{1,0:T(8,128)(2,1)} %v_hbm.1, bf16[2,128,2048]{2,1,0:T(8,128)(2,1)} %past_hbm.1), custom_call_target="tpu_custom_call" | custom-call | tf_op jit(solution)/shard_map/attention/pallas_call | solution.py:433
  57.9 0.8 %copy.8 = bf16[128,2048]{1,0:T(8,128)(2,1)} copy(bf16[128,2048]{1,0:T(8,128)(2,1)S(1)} %attention.1) | data formatting | bytes 1048576

commit v6 on v5

--- a/solution.py
+++ b/solution.py
@@ -21,18 +21,19 @@
 MODES = ((1, 2), (0, 3))
 RAISED = next(h for h, (up_hops, _down_hops) in enumerate(MODES) if up_hops)
 EXCHANGE = (
-    9, 11, 10, 14, 15, 25, 7, 2, 6, 19, 1, 34, 39, 22, 4, 47, 29, 27, 43, 44, 31, 26, 13, 5,
-    12, 20, 18, 35, 28, 42, 3, 45, 30, 46, 41, 37, 38, 21, 36, 33, 23, 17,
+    25, 26, 27, 28, 29, 30, 31, 41, 42, 43, 44, 45, 46, 47, 9, 10, 11, 12, 13, 14, 15, 17, 18, 19,
+    20, 21, 22, 23, 33, 34, 35, 36, 37, 38, 39, 1, 2, 3, 4, 5, 6, 7,
 )
 
-STEPS = ("S0", "R1", "R2", "C3", "C2", "C1", "C0", "M2", "M1", "M0", "KV", "KF", "SK", "XK", "XI")
+STEPS = ("S0", "R1", "R2", "C3", "C2", "C1", "C0", "M2", "M1", "M0", "KV", "KF", "SK", "XK", "XI", "FL")
 ORDER = (
-    224, 0, 8, 193, 9, 11, 196, 197, 226, 194, 10, 192, 14, 228, 15, 227, 195, 199, 24, 25, 27, 26, 225, 30,
-    31, 40, 41, 43, 42, 198, 46, 47, 161, 87, 13, 215, 210, 213, 229, 12, 5, 4, 84, 7, 52, 6, 53, 55,
-    29, 1, 68, 69, 28, 71, 211, 212, 121, 214, 122, 120, 126, 20, 209, 21, 103, 23, 102, 127, 100, 22, 123, 101,
-    137, 45, 160, 85, 44, 138, 98, 142, 70, 143, 3, 176, 16, 50, 139, 2, 66, 82, 17, 117, 67, 116, 51, 118,
-    158, 54, 19, 119, 86, 153, 96, 18, 133, 99, 83, 132, 64, 48, 81, 134, 80, 125, 113, 124, 65, 49, 135, 115,
-    150, 114, 129, 140, 97, 141, 154, 151, 131, 159, 155, 130, 148, 112, 145, 149, 157, 136, 156, 147, 146, 128, 152, 144,
+    15, 196, 199, 195, 11, 197, 198, 192, 194, 10, 14, 12, 13, 8, 9, 224, 225, 226, 27, 26, 31, 30, 212, 28,
+    193, 29, 43, 214, 213, 42, 47, 46, 215, 161, 44, 69, 45, 24, 71, 1, 211, 25, 7, 5, 6, 0, 85, 4,
+    227, 53, 240, 55, 240, 54, 240, 122, 228, 3, 86, 210, 70, 123, 240, 126, 209, 40, 103, 68, 41, 100, 127, 101,
+    87, 23, 2, 124, 240, 22, 17, 125, 16, 139, 142, 21, 138, 102, 84, 229, 143, 20, 52, 240, 19, 141, 158, 140,
+    160, 155, 67, 176, 51, 118, 83, 120, 154, 119, 18, 80, 121, 159, 50, 66, 64, 48, 116, 156, 113, 117, 81, 157,
+    82, 65, 134, 49, 135, 99, 115, 114, 98, 240, 129, 137, 133, 132, 97, 150, 240, 151, 131, 130, 96, 145, 112, 136,
+    153, 149, 148, 147, 146, 128, 152, 144,
 )
 
 
@@ -49,14 +50,13 @@
     slot_hbm, table_hbm, q_hbm, k_hbm, v_hbm, past_hbm, out,
     slot, table, qs, ks, vs, past, base, tally,
     qb, kb, vb, vt, q1, q2, q3, raised, kf, vf, vft, o_in, l_in, o_out, l_out, acc, top, tot, scores, ready, came,
-    stage_sem, ex_send, q_ex, kv_ex, q_send, q_recv, kv_send, raised_recv, kf_recv, o_send, f_send, f_recv,
+    stage_sem, ex_send, q_ex, kv_ex, q_send, q_recv, kv_send, raised_recv, kf_recv, o_send, o_recv, f_send, f_recv,
 ):
     z = lax.axis_index("seq")
     n_z = lax.axis_size("seq")
     me = lax.axis_index("uly")
     y, x = me // 4, lax.rem(me, 4)
     below, above = z > 0, z < n_z - 1
-    far_below = below
     to_lower = {"seq": jnp.maximum(z - 1, 0)}
     to_upper = {"seq": jnp.minimum(z + 1, n_z - 1)}
 
@@ -83,25 +83,25 @@
 
     @pl.when(above)
     def _():
-        pl.semaphore_signal(barrier, inc=1, device_id=to_upper, device_id_type=MESH)
+        for p in range(8):
+            upper = {"seq": jnp.minimum(z + 1, n_z - 1), "uly": peer(p)}
+            pl.semaphore_signal(barrier, inc=1, device_id=upper, device_id_type=MESH)
 
     gathered = ((q_hbm, qs, qb), (k_hbm, ks, kb), (v_hbm, vs, vb))
 
-    def exchange_sem(t, h, p):
-        if t == 0:
-            return q_ex.at[h, p]
-        return kv_ex.at[h]
+    def exchange_sem(t, h):
+        return (q_ex if t == 0 else kv_ex).at[h]
 
     def own_copy(t, h):
         src, _staged, dst = gathered[t]
-        return pltpu.make_async_copy(src.at[:, columns_of(me, h)], dst.at[h, place_rows(0)], exchange_sem(t, h, 0))
+        return pltpu.make_async_copy(src.at[:, columns_of(me, h)], dst.at[h, place_rows(0)], exchange_sem(t, h))
 
     def exchange(t, h, p):
         _src, staged, dst = gathered[t]
         to = peer(MIRROR[p])
         return pltpu.make_async_remote_copy(
             src_ref=staged.at[:, columns_of(to, h)], dst_ref=dst.at[h, place_rows(p)],
-            send_sem=ex_send.at[0], recv_sem=exchange_sem(t, h, p), device_id={"uly": to}, device_id_type=MESH,
+            send_sem=ex_send.at[0], recv_sem=exchange_sem(t, h), device_id={"uly": to}, device_id_type=MESH,
         )
 
     def stage(t):
@@ -137,7 +137,7 @@
 
         lax.fori_loop(0, 8, rows_sum, 0)
 
-    pl.semaphore_wait(barrier, 7 + jnp.where(far_below, 1, 0) + jnp.where(above, 1, 0))
+    pl.semaphore_wait(barrier, 7 + jnp.where(below, 8, 0) + jnp.where(above, 1, 0))
 
     blocks = (qb, q1, q2, q3)
 
@@ -149,8 +149,16 @@
 
     def query_sem(level, chunk):
         if level == 0:
-            return q_ex.at[chunk // 8, chunk % 8]
+            return o_recv.at[chunk]
         return q_recv.at[(level - 1) * 16 + chunk - chunk_base(level - 1)]
+
+    def lower_piece(chunk):
+        h, rows = split(chunk)
+        to = peer(MIRROR[chunk % 8])
+        return pltpu.make_async_remote_copy(
+            src_ref=qs.at[:, columns_of(to, h)], dst_ref=q1.at[h, rows], send_sem=q_send.at[0],
+            recv_sem=query_sem(1, chunk), device_id={"seq": jnp.maximum(z - 1, 0), "uly": to}, device_id_type=MESH,
+        )
 
     def down(level, chunk):
         h, rows = split(chunk)
@@ -217,6 +225,9 @@
     came_up = [below, has(1) & below, has(2) & below]
 
     def queries(level, chunk):
+        if level == 0:
+            h = chunk // 8
+            return (None, ("own", h), [functools.partial(arrived, q_ex.at[h], 512)])
         return (exists[level], ("down", level, chunk), [functools.partial(arrived, query_sem(level, chunk), 64)])
 
     def part(level, chunk):
@@ -319,18 +330,16 @@
         weighted = acc[level, pair, :, lanes] * a + new_weighted * b
         return weighted / total, most + jnp.log2(total)
 
-    held = None
-
     def run(step, which):
-        nonlocal held
-        if step in ("S0", "R1", "R2"):
-            level = STEPS.index(step)
+        if step == "S0":
+            expect(in_vmem(0))
+            pl.when(below)(lower_piece(which).start)
+        elif step in ("R1", "R2"):
+            level = int(step[1])
             expect(queries(level, which))
-            if held is None:
-                pl.when(has(level) & below)(down(level, which).start)
-            else:
-                pl.when(has(level) & far_below)(down(level, which).start)
-                held.append((level, which))
+            pl.when(has(level) & below)(down(level, which).start)
+        elif step == "FL":
+            advance()
         elif step == "XI":
             for code in EXCHANGE[which * 7 : which * 7 + 7]:
                 expect(in_vmem(code // 16))
@@ -349,11 +358,6 @@
             def _():
                 for t in (1, 2):
                     pass_on(t, which).start()
-
-            if held is not None:
-                for level, chunk in held:
-                    pl.when(has(level) & (z == 1))(down(level, chunk).start)
-                held = None
         elif step == "KV":
             expect((None, ("keys", which), [functools.partial(arrived, kv_ex.at[which], 1024)]))
             vt[which] = jnp.transpose(vb[which])
@@ -395,7 +399,7 @@
     summed = False
     for code in ORDER:
         step, which = STEPS[code // 16], code % 16
-        if not summed and step not in ("XI", "SK") and which % 8:
+        if not summed and step not in ("XI", "SK", "S0"):
             pl.when(z == 0)(no_parts)
             stored_sum()
             summed = True
@@ -442,8 +446,8 @@
             pltpu.VMEM(parts, BF16), pltpu.VMEM(logs, F32), pltpu.VMEM(parts, BF16), pltpu.VMEM(logs, F32),
             pltpu.VMEM((4, 8, HEAD_DIM, 256), F32), pltpu.VMEM((4, 8, 1, 256), F32), pltpu.VMEM((4, 8, 1, 256), F32),
             pltpu.VMEM((2, 1024, 256), F32), block, pltpu.VMEM((8, 2, 128, HEAD_DIM), BF16),
-            dma((6,)), dma((2,)), dma((2, 8)), dma((2,)), dma((3,)), dma((chunks,)), dma(()), dma((8,)), dma(()),
-            dma((3,)), dma(()), dma((len(BATCHES),)),
+            dma((6,)), dma((2,)), dma((2,)), dma((2,)), dma((3,)), dma((chunks,)), dma(()), dma((8,)), dma(()),
+            dma((3,)), dma((16,)), dma(()), dma((len(BATCHES),)),
         ],
         compiler_params=pltpu.CompilerParams(collective_id=0, has_side_effects=True),
         name="attention",

time: 58.8 us -> 58.7 us (level)
  the two profiles are of different devices: /device:TPU:64 before, /device:TPU:32 now
where the time goes in v6:
time: 58.7 us; the launch traced here: 58.5 us
  Pallas kernels  57.7 us (98%)
  local copies, waits for them, and re-layouts  0.8 us (1%)
    pallas_call x1, Pallas kernels, attention(): pl.pallas_call(kernel, out_shape=pltpu.VMEM(queries.shape, BF16), in_spec...  57.7 us

profile of v6, /device:TPU:32, one launch (start us, length us, event | category | flops | bytes accessed | tf_op | source)
XLA Modules:
  0.0 58.5 jit_solution(10035684051876326210)
XLA Ops:
  0.0 57.7 %attention.1 = bf16[128,2048]{1,0:T(8,128)(2,1)S(1)} custom-call(s32[2]{0:T(128)} %slot_hbm.1, f32[2,64]{1,0:T(2,128)} %table_hbm.1, bf16[128,2048]{1,0:T(8,128)(2,1)} %q_hbm.1, bf16[128,2048]{1,0:T(8,128)(2,1)} %k_hbm.1, bf16[128,2048]{1,0:T(8,128)(2,1)} %v_hbm.1, bf16[2,128,2048]{2,1,0:T(8,128)(2,1)} %past_hbm.1), custom_call_target="tpu_custom_call" | custom-call | tf_op jit(solution)/shard_map/attention/pallas_call | solution.py:437
  57.7 0.8 %copy.8 = bf16[128,2048]{1,0:T(8,128)(2,1)} copy(bf16[128,2048]{1,0:T(8,128)(2,1)S(1)} %attention.1) | data formatting | bytes 1048576

commit v7 on v6

--- a/solution.py
+++ b/solution.py
@@ -36,6 +36,8 @@
     153, 149, 148, 147, 146, 128, 152, 144,
 )
 
+
+PAUSES = {STEPS.index("M2") * 16 + 10: 2000}
 
 M0S = tuple(code % 16 for code in ORDER if STEPS[code // 16] == "M0")
 BATCHES = ((0, 8), (8, 11), (11, 13), (13, 14), (14, 15), (15, 16))
@@ -403,6 +405,9 @@
             pl.when(z == 0)(no_parts)
             stored_sum()
             summed = True
+        ns = PAUSES.get(code)
+        if ns:
+            pl.when(lax.rem(lax.axis_index("rep"), 2) == 1)(functools.partial(pl.delay, ns))
         run(step, which)
 
     for batch, (first, last) in enumerate(BATCHES):

time: 58.7 us -> 57.4 us (0.978)
  the two profiles are of different devices: /device:TPU:32 before, /device:TPU:64 now
where the time goes in v7:
time: 57.4 us; the launch traced here: 57 us
  Pallas kernels  56.2 us (98%)
  local copies, waits for them, and re-layouts  0.8 us (1%)
    pallas_call x1, Pallas kernels, attention(): pl.pallas_call(kernel, out_shape=pltpu.VMEM(queries.shape, BF16), in_spec...  56.2 us

profile of v7, /device:TPU:64, one launch (start us, length us, event | category | flops | bytes accessed | tf_op | source)
XLA Modules:
  0.0 57.0 jit_solution(713738360657603624)
XLA Ops:
  0.0 56.2 %attention.1 = bf16[128,2048]{1,0:T(8,128)(2,1)S(1)} custom-call(s32[2]{0:T(128)} %slot_hbm.1, f32[2,64]{1,0:T(2,128)} %table_hbm.1, bf16[128,2048]{1,0:T(8,128)(2,1)} %q_hbm.1, bf16[128,2048]{1,0:T(8,128)(2,1)} %k_hbm.1, bf16[128,2048]{1,0:T(8,128)(2,1)} %v_hbm.1, bf16[2,128,2048]{2,1,0:T(8,128)(2,1)} %past_hbm.1), custom_call_target="tpu_custom_call" | custom-call | tf_op jit(solution)/shard_map/attention/pallas_call | solution.py:442
  56.2 0.8 %copy.8 = bf16[128,2048]{1,0:T(8,128)(2,1)} copy(bf16[128,2048]{1,0:T(8,128)(2,1)S(1)} %attention.1) | data formatting | bytes 1048576

commit v8 on v7

--- a/solution.py
+++ b/solution.py
@@ -21,26 +21,28 @@
 MODES = ((1, 2), (0, 3))
 RAISED = next(h for h, (up_hops, _down_hops) in enumerate(MODES) if up_hops)
 EXCHANGE = (
-    25, 26, 27, 28, 29, 30, 31, 41, 42, 43, 44, 45, 46, 47, 9, 10, 11, 12, 13, 14, 15, 17, 18, 19,
-    20, 21, 22, 23, 33, 34, 35, 36, 37, 38, 39, 1, 2, 3, 4, 5, 6, 7,
+    25, 26, 27, 28, 29, 30, 31, 41, 42, 43, 44, 45, 46, 47, 17, 18, 19, 20, 21, 22, 23, 33, 34, 35,
+    36, 37, 38, 39, 9, 10, 11, 12, 13, 14, 15, 1, 2, 3, 4, 5, 6, 7,
 )
 
 STEPS = ("S0", "R1", "R2", "C3", "C2", "C1", "C0", "M2", "M1", "M0", "KV", "KF", "SK", "XK", "XI", "FL")
+DIRECT = (1, 2, 3, 9)
 ORDER = (
-    15, 196, 199, 195, 11, 197, 198, 192, 194, 10, 14, 12, 13, 8, 9, 224, 225, 226, 27, 26, 31, 30, 212, 28,
-    193, 29, 43, 214, 213, 42, 47, 46, 215, 161, 44, 69, 45, 24, 71, 1, 211, 25, 7, 5, 6, 0, 85, 4,
-    227, 53, 240, 55, 240, 54, 240, 122, 228, 3, 86, 210, 70, 123, 240, 126, 209, 40, 103, 68, 41, 100, 127, 101,
-    87, 23, 2, 124, 240, 22, 17, 125, 16, 139, 142, 21, 138, 102, 84, 229, 143, 20, 52, 240, 19, 141, 158, 140,
-    160, 155, 67, 176, 51, 118, 83, 120, 154, 119, 18, 80, 121, 159, 50, 66, 64, 48, 116, 156, 113, 117, 81, 157,
-    82, 65, 134, 49, 135, 99, 115, 114, 98, 240, 129, 137, 133, 132, 97, 150, 240, 151, 131, 130, 96, 145, 112, 136,
-    153, 149, 148, 147, 146, 128, 152, 144,
+    12, 192, 13, 197, 199, 196, 15, 195, 193, 11, 194, 10, 14, 198, 9, 224, 225, 226, 28, 29, 27, 26, 31, 215,
+    30, 212, 44, 45, 43, 42, 210, 47, 46, 6, 7, 8, 4, 25, 161, 0, 5, 209, 69, 70, 227, 54, 240, 53,
+    240, 55, 240, 124, 1, 213, 86, 2, 240, 122, 214, 24, 3, 125, 22, 71, 87, 84, 23, 85, 211, 123, 228, 126,
+    20, 240, 140, 21, 127, 141, 160, 40, 138, 68, 41, 80, 16, 17, 142, 83, 82, 139, 67, 176, 18, 143, 51, 119,
+    229, 118, 19, 66, 50, 116, 81, 117, 52, 101, 103, 154, 135, 159, 134, 102, 155, 158, 48, 65, 156, 133, 157, 132,
+    49, 64, 113, 121, 114, 99, 98, 151, 150, 120, 115, 100, 149, 96, 240, 129, 112, 137, 148, 130, 131, 97, 136, 240,
+    145, 128, 146, 153, 147, 152, 144,
 )
 
 
-PAUSES = {STEPS.index("M2") * 16 + 10: 2000}
-
-M0S = tuple(code % 16 for code in ORDER if STEPS[code // 16] == "M0")
-BATCHES = ((0, 8), (8, 11), (11, 13), (13, 14), (14, 15), (15, 16))
+PAUSES = {STEPS.index("M2") * 16 + 12: 2000}
+LATE_PAUSES = {STEPS.index("M2") * 16 + 12: 2000}
+
+M0S = tuple(code % 16 for code in ORDER if STEPS[code // 16] == "M0" and code % 16 not in DIRECT)
+BATCHES = ((0, 8), (8, len(M0S) - 2), (len(M0S) - 2, len(M0S) - 1), (len(M0S) - 1, len(M0S)))
 
 
 def batch_of(chunk):
@@ -52,7 +54,8 @@
     slot_hbm, table_hbm, q_hbm, k_hbm, v_hbm, past_hbm, out,
     slot, table, qs, ks, vs, past, base, tally,
     qb, kb, vb, vt, q1, q2, q3, raised, kf, vf, vft, o_in, l_in, o_out, l_out, acc, top, tot, scores, ready, came,
-    stage_sem, ex_send, q_ex, kv_ex, q_send, q_recv, kv_send, raised_recv, kf_recv, o_send, o_recv, f_send, f_recv,
+    part_out, part_log_out, part_in, part_log_in,
+    stage_sem, ex_send, q_ex, kv_ex, q_send, q_recv, kv_send, raised_recv, kf_recv, o_send, o_recv, f_send, f_recv, part_send, part_recv,
 ):
     z = lax.axis_index("seq")
     n_z = lax.axis_size("seq")
@@ -124,6 +127,8 @@
     def no_parts():
         o_in[...] = jnp.zeros_like(o_in)
         l_in[...] = jnp.full_like(l_in, -1e30)
+        part_in[1] = jnp.zeros(part_in.shape[1:], BF16)
+        part_log_in[1] = jnp.full(part_log_in.shape[1:], -1e30, F32)
         kf[...] = jnp.zeros_like(kf)
         vf[...] = jnp.zeros_like(vf)
 
@@ -185,12 +190,27 @@
         )
 
     def up(level, chunk):
+        to, recv, targets = to_upper, query_sem(level, chunk), (o_in.at[level, chunk], l_in.at[level, chunk])
+        if level == 0 and chunk in DIRECT:
+            at = chunk // 8 * 8 + MIRROR[chunk % 8]
+            to = {"seq": to_upper["seq"], "uly": peer(chunk % 8)}
+            recv, targets = part_recv.at[at], (part_in.at[1, at], part_log_in.at[1, at])
         return [
             pltpu.make_async_remote_copy(
-                src_ref=src.at[level, chunk], dst_ref=dst.at[level, chunk],
-                send_sem=o_send.at[level], recv_sem=query_sem(level, chunk), device_id=to_upper, device_id_type=MESH,
+                src_ref=src.at[level, chunk], dst_ref=dst, send_sem=o_send.at[level], recv_sem=recv, device_id=to,
+                device_id_type=MESH,
             )
-            for src, dst in ((o_out, o_in), (l_out, l_in))
+            for src, dst in zip((o_out, l_out), targets)
+        ]
+
+    def own_part(chunk):
+        at = chunk // 8 * 8 + MIRROR[chunk % 8]
+        return [
+            pltpu.make_async_remote_copy(
+                src_ref=src.at[chunk], dst_ref=dst.at[0, at], send_sem=part_send, recv_sem=part_recv.at[at],
+                device_id={"uly": peer(chunk % 8)}, device_id_type=MESH,
+            )
+            for src, dst in ((part_out, part_in), (part_log_out, part_log_in))
         ]
 
     def arrived(semaphore, count):
@@ -300,6 +320,13 @@
             else:
                 acc[old, old_pair] = weighted
                 tot[old, old_pair] = total
+                for chunk in (2 * old_pair, 2 * old_pair + 1):
+                    if old == 0 and chunk in DIRECT:
+                        lanes = slice(chunk % 2 * 128, chunk % 2 * 128 + 128)
+                        part_out[chunk] = (weighted / total)[:, lanes].astype(BF16)
+                        part_log_out[chunk] = (old_top * SCALE + jnp.log2(total))[:, lanes]
+                        for copy in own_part(chunk):
+                            copy.start()
                 if old == 3:
                     top[old, old_pair] = jnp.where(below, old_top, -1e30)
         if step is not None:
@@ -372,6 +399,18 @@
                 level = 2
             expect(queries(level, 2 * which), queries(level, 2 * which + 1))
             advance(step, which)
+        elif step == "M0" and which in DIRECT:
+            settle(("C0", which // 2))
+            h, place = which // 8, MIRROR[which % 8]
+            at = h * 8 + place
+            pl.when(below)(functools.partial(arrived, part_recv.at[at], 130))
+            pl.when(z == 0)(functools.partial(arrived, part_recv.at[at], 65))
+            most = jnp.maximum(part_log_in[0, at], part_log_in[1, at])
+            a, b = (jnp.exp2(part_log_in[i, at] - most) for i in range(2))
+            mean = (part_in[0, at].astype(F32) * a + part_in[1, at].astype(F32) * b) / (a + b)
+            attended = jnp.transpose(mean).astype(BF16).astype(F32)
+            lanes = columns_of(peer(place), h)
+            out[:, lanes] = (base[:, lanes] + attended).astype(BF16)
         elif step == "M0":
             settle(("C0", which // 2))
             expect(part(0, which))
@@ -408,6 +447,9 @@
         ns = PAUSES.get(code)
         if ns:
             pl.when(lax.rem(lax.axis_index("rep"), 2) == 1)(functools.partial(pl.delay, ns))
+        ns = LATE_PAUSES.get(code)
+        if ns:
+            pl.when((lax.axis_index("rep") == 1) & (z < 4))(functools.partial(pl.delay, ns))
         run(step, which)
 
     for batch, (first, last) in enumerate(BATCHES):
@@ -422,8 +464,9 @@
 
     sent = scores.at[:, pl.ds(0, 672)]
     pltpu.make_async_copy(sent, sent, ex_send.at[0]).wait()
-    sent = ready.at[:, pl.ds(0, 896)]
-    pltpu.make_async_copy(sent, sent, f_send).wait()
+    arrived(f_send, 64 * (14 - len(DIRECT)))
+    if DIRECT:
+        arrived(part_send, 65 * len(DIRECT))
     pl.when(below)(functools.partial(arrived, ex_send.at[1], 896))
     pl.when(above)(functools.partial(arrived, kv_send, 1024))
     for level in range(3):
@@ -451,8 +494,10 @@
             pltpu.VMEM(parts, BF16), pltpu.VMEM(logs, F32), pltpu.VMEM(parts, BF16), pltpu.VMEM(logs, F32),
             pltpu.VMEM((4, 8, HEAD_DIM, 256), F32), pltpu.VMEM((4, 8, 1, 256), F32), pltpu.VMEM((4, 8, 1, 256), F32),
             pltpu.VMEM((2, 1024, 256), F32), block, pltpu.VMEM((8, 2, 128, HEAD_DIM), BF16),
+            pltpu.VMEM(parts[1:], BF16), pltpu.VMEM(logs[1:], F32),
+            pltpu.VMEM((2, *parts[1:]), BF16), pltpu.VMEM((2, *logs[1:]), F32),
             dma((6,)), dma((2,)), dma((2,)), dma((2,)), dma((3,)), dma((chunks,)), dma(()), dma((8,)), dma(()),
-            dma((3,)), dma((16,)), dma(()), dma((len(BATCHES),)),
+            dma((3,)), dma((16,)), dma(()), dma((len(BATCHES),)), dma(()), dma((16,)),
         ],
         compiler_params=pltpu.CompilerParams(collective_id=0, has_side_effects=True),
         name="attention",

time: 57.4 us -> 57 us (level)
  the two profiles are of different devices: /device:TPU:64 before, /device:TPU:98 now
where the time goes in v8:
time: 57 us; the launch traced here: 56.8 us
  Pallas kernels  56 us (98%)
  local copies, waits for them, and re-layouts  0.8 us (1%)
    pallas_call x1, Pallas kernels, attention(): pl.pallas_call(kernel, out_shape=pltpu.VMEM(queries.shape, BF16), in_spec...  56 us

profile of v8, /device:TPU:98, one launch (start us, length us, event | category | flops | bytes accessed | tf_op | source)
XLA Modules:
  0.0 56.8 jit_solution(11077319928388154301)
XLA Ops:
  0.0 56.0 %attention.1 = bf16[128,2048]{1,0:T(8,128)(2,1)S(1)} custom-call(s32[2]{0:T(128)} %slot_hbm.1, f32[2,64]{1,0:T(2,128)} %table_hbm.1, bf16[128,2048]{1,0:T(8,128)(2,1)} %q_hbm.1, bf16[128,2048]{1,0:T(8,128)(2,1)} %k_hbm.1, bf16[128,2048]{1,0:T(8,128)(2,1)} %v_hbm.1, bf16[2,128,2048]{2,1,0:T(8,128)(2,1)} %past_hbm.1), custom_call_target="tpu_custom_call" | custom-call | tf_op jit(solution)/shard_map/attention/pallas_call | solution.py:485
  56.0 0.8 %copy.8 = bf16[128,2048]{1,0:T(8,128)(2,1)} copy(bf16[128,2048]{1,0:T(8,128)(2,1)S(1)} %attention.1) | data formatting | bytes 1048576

commit v9 on v8

--- a/solution.py
+++ b/solution.py
@@ -40,6 +40,8 @@
 
 PAUSES = {STEPS.index("M2") * 16 + 12: 2000}
 LATE_PAUSES = {STEPS.index("M2") * 16 + 12: 2000}
+
+PARTS_AT = tuple(chunk // 8 * 8 + MIRROR[chunk % 8] for chunk in DIRECT)
 
 M0S = tuple(code % 16 for code in ORDER if STEPS[code // 16] == "M0" and code % 16 not in DIRECT)
 BATCHES = ((0, 8), (8, len(M0S) - 2), (len(M0S) - 2, len(M0S) - 1), (len(M0S) - 1, len(M0S)))
@@ -194,7 +196,7 @@
         if level == 0 and chunk in DIRECT:
             at = chunk // 8 * 8 + MIRROR[chunk % 8]
             to = {"seq": to_upper["seq"], "uly": peer(chunk % 8)}
-            recv, targets = part_recv.at[at], (part_in.at[1, at], part_log_in.at[1, at])
+            recv, targets = part_recv.at[PARTS_AT.index(at)], (part_in.at[1, at], part_log_in.at[1, at])
         return [
             pltpu.make_async_remote_copy(
                 src_ref=src.at[level, chunk], dst_ref=dst, send_sem=o_send.at[level], recv_sem=recv, device_id=to,
@@ -207,7 +209,7 @@
         at = chunk // 8 * 8 + MIRROR[chunk % 8]
         return [
             pltpu.make_async_remote_copy(
-                src_ref=src.at[chunk], dst_ref=dst.at[0, at], send_sem=part_send, recv_sem=part_recv.at[at],
+                src_ref=src.at[chunk], dst_ref=dst.at[0, at], send_sem=part_send, recv_sem=part_recv.at[PARTS_AT.index(at)],
                 device_id={"uly": peer(chunk % 8)}, device_id_type=MESH,
             )
             for src, dst in ((part_out, part_in), (part_log_out, part_log_in))
@@ -403,8 +405,8 @@
             settle(("C0", which // 2))
             h, place = which // 8, MIRROR[which % 8]
             at = h * 8 + place
-            pl.when(below)(functools.partial(arrived, part_recv.at[at], 130))
-            pl.when(z == 0)(functools.partial(arrived, part_recv.at[at], 65))
+            pl.when(below)(functools.partial(arrived, part_recv.at[PARTS_AT.index(at)], 130))
+            pl.when(z == 0)(functools.partial(arrived, part_recv.at[PARTS_AT.index(at)], 65))
             most = jnp.maximum(part_log_in[0, at], part_log_in[1, at])
             a, b = (jnp.exp2(part_log_in[i, at] - most) for i in range(2))
             mean = (part_in[0, at].astype(F32) * a + part_in[1, at].astype(F32) * b) / (a + b)
@@ -449,7 +451,7 @@
             pl.when(lax.rem(lax.axis_index("rep"), 2) == 1)(functools.partial(pl.delay, ns))
         ns = LATE_PAUSES.get(code)
         if ns:
-            pl.when((lax.axis_index("rep") == 1) & (z < 4))(functools.partial(pl.delay, ns))
+            pl.when((lax.axis_index("rep") == 1) & (z < 8))(functools.partial(pl.delay, ns))
         run(step, which)
 
     for batch, (first, last) in enumerate(BATCHES):
@@ -497,7 +499,7 @@
             pltpu.VMEM(parts[1:], BF16), pltpu.VMEM(logs[1:], F32),
             pltpu.VMEM((2, *parts[1:]), BF16), pltpu.VMEM((2, *logs[1:]), F32),
             dma((6,)), dma((2,)), dma((2,)), dma((2,)), dma((3,)), dma((chunks,)), dma(()), dma((8,)), dma(()),
-            dma((3,)), dma((16,)), dma(()), dma((len(BATCHES),)), dma(()), dma((16,)),
+            dma((3,)), dma((16,)), dma(()), dma((len(BATCHES),)), dma(()), dma((len(DIRECT),)),
         ],
         compiler_params=pltpu.CompilerParams(collective_id=0, has_side_effects=True),
         name="attention",

time: 57 us -> 56.9 us (level)
  no operation moved by 1% of the time
where the time goes in v9:
time: 56.9 us; the launch traced here: 56.7 us
  Pallas kernels  55.9 us (98%)
  local copies, waits for them, and re-layouts  0.8 us (1%)
    pallas_call x1, Pallas kernels, attention(): pl.pallas_call(kernel, out_shape=pltpu.VMEM(queries.shape, BF16), in_spec...  55.9 us

profile of v9, /device:TPU:98, one launch (start us, length us, event | category | flops | bytes accessed | tf_op | source)
XLA Modules:
  0.0 56.7 jit_solution(15610576616305404007)
XLA Ops:
  0.0 55.9 %attention.1 = bf16[128,2048]{1,0:T(8,128)(2,1)S(1)} custom-call(s32[2]{0:T(128)} %slot_hbm.1, f32[2,64]{1,0:T(2,128)} %table_hbm.1, bf16[128,2048]{1,0:T(8,128)(2,1)} %q_hbm.1, bf16[128,2048]{1,0:T(8,128)(2,1)} %k_hbm.1, bf16[128,2048]{1,0:T(8,128)(2,1)} %v_hbm.1, bf16[2,128,2048]{2,1,0:T(8,128)(2,1)} %past_hbm.1), custom_call_target="tpu_custom_call" | custom-call | tf_op jit(solution)/shard_map/attention/pallas_call | solution.py:487
  55.9 0.8 %copy.8 = bf16[128,2048]{1,0:T(8,128)(2,1)} copy(bf16[128,2048]{1,0:T(8,128)(2,1)S(1)} %attention.1) | data formatting | bytes 1048576
